TPU v7x, 32 devices: a whole 2x2x4 slice. The times are simulated.
32 devices in a mesh: beta: 16 (over z, y, x), grp: 2 (over core).
Axes of the slice: x: 2, y: 2, z: 4, core: 2. Of those that a mesh axis runs over, the one named last changes fastest.
Arguments:
- samples: float32 [128, 8, 128, 128], P('beta', 'grp'), parts along dimension 1, may hold values from -6 to 6
Outputs:
- coeffs: float32 [128, 2, 8, 64, 64], P('beta', None, 'grp'), parts along dimension 2
- power: float32 [8, 64], P('grp'), parts along dimension 0
There are 2 independent parts, one for each index of `grp`. A program takes and returns all parts, laid end to end along the dimension named above; each array names one. Nothing has to cross between parts.
All inputs are finite; a program needn't handle non-finite values.
Results may differ from a plain program's by a relative error of at most 0.0003.
Values sent between devices are 32-bit elements; how exact they have to be, the bound alone decides.
No kernel may reach another device: no remote copies, remote signals or barrier semaphores. Data moves between devices by JAX's collectives and lax.ppermute only.
A program may use at most 64 MiB of HBM per device.

v0:
```python
import jax
import jax.numpy as jnp
from jax import lax
from jax.sharding import PartitionSpec as P

HIGHEST = lax.Precision.HIGHEST


def beta_angles(spread):
    grid_size = 2 * spread
    return (2.0 * jnp.arange(grid_size, dtype=jnp.float32) + 1.0) * (jnp.pi / (4.0 * spread))


def quadrature(spread):
    angles = beta_angles(spread)
    odd_terms = 2.0 * jnp.arange(spread, dtype=jnp.float32) + 1.0
    series = jnp.sum(jnp.sin(angles[:, None] * odd_terms[None, :]) / odd_terms[None, :], axis=1)
    return 2.0 / spread * jnp.sin(angles) * series


def gamma_table(spread):
    grid_size = 2 * spread
    positions = jnp.arange(grid_size, dtype=jnp.int32)
    orders = jnp.arange(spread, dtype=jnp.int32)
    phase_index = positions[:, None] * orders[None, :] % grid_size
    angles = phase_index.astype(jnp.float32) * (2.0 * jnp.pi / grid_size)
    return jnp.concatenate([jnp.cos(angles), -jnp.sin(angles)], axis=1)


def alpha_table(spread, row_index):
    grid_size = 2 * spread
    positions = jnp.arange(grid_size, dtype=jnp.int32)
    phase_index = row_index[:, None] * positions[None, :] % grid_size
    angles = phase_index.astype(jnp.float32) * (2.0 * jnp.pi / grid_size)
    cosine = jnp.cos(angles) / grid_size
    sine_part = jnp.sin(angles) / grid_size
    real_rows = jnp.stack([cosine, sine_part], axis=1)
    imag_rows = jnp.stack([-sine_part, cosine], axis=1)
    return jnp.stack([real_rows, imag_rows], axis=0)


def log_factorial(value, float_type):
    return lax.lgamma((value + 1).astype(float_type))


def wigner_start(alpha_order, gamma_order, log_cosine, log_sine):
    float_type = log_cosine.dtype
    lowest = jnp.maximum(jnp.abs(alpha_order), gamma_order)
    shift_low = jnp.maximum(0, gamma_order - alpha_order)
    magnitude = 0.5 * (
        log_factorial(lowest + alpha_order, float_type)
        + log_factorial(lowest - alpha_order, float_type)
        + log_factorial(lowest + gamma_order, float_type)
        + log_factorial(lowest - gamma_order, float_type)
    )
    magnitude = (
        magnitude
        - log_factorial(lowest + gamma_order - shift_low, float_type)
        - log_factorial(shift_low, float_type)
    )
    magnitude = magnitude - log_factorial(alpha_order - gamma_order + shift_low, float_type)
    magnitude = magnitude - log_factorial(lowest - alpha_order - shift_low, float_type)
    cos_power = (2 * lowest + gamma_order - alpha_order - 2 * shift_low).astype(float_type)
    sin_power = (alpha_order - gamma_order + 2 * shift_low).astype(float_type)
    parity = (alpha_order - gamma_order + shift_low) % 2
    sign_factor = (1 - 2 * parity).astype(float_type)
    return sign_factor * jnp.exp(magnitude + cos_power * log_cosine + sin_power * log_sine)


def advance(degree, carried, alpha_order, gamma_order, cos_angles, start_value, lowest):
    former, current = carried
    float_type = current.dtype
    previous = (degree - 1).astype(float_type)
    alpha_float = alpha_order.astype(float_type)
    gamma_float = gamma_order.astype(float_type)
    cross_ratio = alpha_float * gamma_float / jnp.maximum(previous * (previous + 1.0), 1.0)
    upper_term = ((previous + 1.0) * (previous + 1.0) - alpha_float * alpha_float) * (
        (previous + 1.0) * (previous + 1.0) - gamma_float * gamma_float
    )
    lower_term = (previous * previous - alpha_float * alpha_float) * (
        previous * previous - gamma_float * gamma_float
    )
    root_upper = jnp.sqrt(jnp.maximum(upper_term, 1.0))
    forward = (previous + 1.0) * (2.0 * previous + 1.0) / root_upper
    backward = (
        (previous + 1.0)
        * jnp.sqrt(jnp.maximum(lower_term, 0.0))
        / (jnp.maximum(previous, 1.0) * root_upper)
    )
    recurred = forward * (cos_angles - cross_ratio) * current - backward * former
    renewed = jnp.where(degree == lowest, start_value, recurred)
    return (current, renewed)


def degree_rows(row_index, weighted, spread):
    stride = 8
    grid_size = 2 * spread
    group_size = row_index.shape[0]
    channels = weighted.shape[2]
    block_count = spread // stride
    alpha_order = jnp.where(row_index < spread, row_index, row_index - grid_size)[:, None, None]
    gamma_order = jnp.arange(spread, dtype=jnp.int32)[None, None, :]
    angles = beta_angles(spread)
    cos_angles = jnp.cos(angles)[None, :, None]
    log_cosine = jnp.log(jnp.cos(0.5 * angles))[None, :, None]
    log_sine = jnp.log(jnp.sin(0.5 * angles))[None, :, None]
    lowest = jnp.maximum(jnp.abs(alpha_order), gamma_order)
    start_value = wigner_start(alpha_order, gamma_order, log_cosine, log_sine)
    first_block = jnp.min(jnp.abs(alpha_order)) // stride
    empty_state = jnp.zeros((group_size, grid_size, spread), jnp.float32)

    def compute_block(operands):
        block_index, former, current = operands
        levels = []
        for offset in range(stride):
            former, current = advance(
                block_index * stride + offset,
                (former, current),
                alpha_order,
                gamma_order,
                cos_angles,
                start_value,
                lowest,
            )
            levels.append(current)
        stacked = jnp.stack(levels, axis=0)
        block_part = jnp.einsum("jgkq,kgcq->gcjq", stacked, weighted, precision=HIGHEST)
        return (former, current, block_part)

    def skip_block(operands):
        block_index, former, current = operands
        return (former, current, jnp.zeros((group_size, channels, stride, spread), jnp.float32))

    def block_step(carried, block_index):
        former, current = carried
        former, current, block_part = lax.cond(
            block_index >= first_block, compute_block, skip_block, (block_index, former, current)
        )
        return ((former, current), block_part)

    _, parts = lax.scan(
        block_step, (empty_state, empty_state), jnp.arange(block_count, dtype=jnp.int32)
    )
    output = jnp.transpose(parts, (1, 2, 0, 3, 4)).reshape(group_size, channels, spread, spread)
    degree_scale = 8.0 * jnp.sqrt(2.0 * jnp.arange(spread, dtype=jnp.float32) + 1.0)
    return output * degree_scale[None, None, :, None]


def degree_energy(coeffs, functions, spread):
    split_view = coeffs.reshape(coeffs.shape[0], 2, functions, spread, spread)
    multiplicity = jnp.where(jnp.arange(spread) == 0, 1.0, 2.0).astype(jnp.float32)
    energy_sum = jnp.sum(split_view * split_view * multiplicity, axis=(0, 1, 4))
    degrees = 2.0 * jnp.arange(spread, dtype=jnp.float32) + 1.0
    return energy_sum / (degrees * degrees)[None, :]


def local(samples):
    devices = lax.axis_size("beta")
    device = lax.axis_index("beta")
    local_beta = samples.shape[0]
    functions = samples.shape[1]
    grid_size = samples.shape[2]
    spread = grid_size // 2
    channels = 2 * functions
    row_count = grid_size // devices
    natural_rows = jnp.arange(grid_size, dtype=jnp.int32)
    halfway = jnp.einsum("kfag,gx->kfax", samples, gamma_table(spread), precision=HIGHEST)
    halfway = halfway.reshape(local_beta, functions, grid_size, 2, spread)
    spectrum = jnp.einsum(
        "kfacq,spca->kpsfq", halfway, alpha_table(spread, natural_rows), precision=HIGHEST
    )
    spectrum = spectrum.reshape(local_beta, grid_size, channels, spread)
    received = lax.all_to_all(spectrum, "beta", split_axis=1, concat_axis=0, tiled=True)
    weighted = received * quadrature(spread)[:, None, None, None]
    owned_rows = lax.dynamic_slice_in_dim(natural_rows, device * row_count, row_count)
    computed = degree_rows(owned_rows, weighted, spread)
    power_part = degree_energy(computed, functions, spread)
    coeffs = computed
    power = lax.psum(power_part, "beta")
    coeffs = coeffs.reshape(row_count, 2, functions, spread, spread)
    return (coeffs, power)


def solution(mesh):
    return jax.shard_map(
        local,
        mesh=mesh,
        in_specs=(P("beta", "grp", None, None),),
        out_specs=(P("beta", None, "grp", None, None), P("grp", None)),
        check_vma=False,
    )
```

profile of v0, /device:TPU:0, one launch (start us, length us, event | category | flops | bytes accessed | tf_op | source)
XLA Modules:
  0.0 345.6 jit_solution(5608972519271680303)
XLA Ops:
  1.4 0.9 copy-done
  2.2 2.0 fusion.27
  4.2 1.9 convolution_bitcast_fusion.1
  6.1 1.6 copy.57
  7.7 5.6 %copy.58 = f32[8,128,8,64]{3,2,0,1:T(8,128)} copy(f32[8,128,8,64]{1,3,2,0:T(8,128)} %bitcast.233) | data formatting | bytes 4194304 | tf_op jit(solution)/shard_map/reshape | solution.py:172
  13.3 5.5 %reshape.2457 = f32[16,1,32768]{2,1,0:T(1,128)} reshape(f32[128,8,8,64]{3,2,1,0:T(8,128)} %bitcast.230) | data formatting | bytes 4194304
  18.8 8.4 %all-to-all-start = ((f32[16,1,32768]{2,1,0:T(1,128)}), f32[16,1,32768]{2,1,0:T(1,128)}, u32[]{:S(2)}, u32[]{:S(2)}) async-start(f32[16,1,32768]{2,1,0:T(1,128)} %reshape.2457), calls=%async_computation | async-start | bytes 4194304 | tf_op jit(solution)/shard_map/all_to_all | solution.py:173
  27.3 0.7 abs_reduce_fusion
  30.8 0.6 fusion.87
  32.1 38.1 %all-to-all-done = f32[16,1,32768]{2,1,0:T(1,128)} async-done(((f32[16,1,32768]{2,1,0:T(1,128)}), f32[16,1,32768]{2,1,0:T(1,128)}, u32[]{:S(2)}, u32[]{:S(2)}) %all-to-all-start) | async-done | bytes 2097184 | tf_op jit(solution)/shard_map/all_to_all | solution.py:173
  70.3 0.6 broadcast.2681
  70.9 8.6 %reduce.3 = f32[16,32768]{1,0:T(8,128)} reduce(f32[16,1,32768]{2,1,0:T(1,128)} %all-to-all-done, f32[]{:T(128)} %broadcast.2681), dimensions={1}, to_apply=%all_to_all.13.reduce_sub_computation | reduce | bytes 4194308 | tf_op jit(solution)/shard_map/all_to_all | solution.py:173
  79.5 4.2 %reshape.2458 = f32[128,8,8,64]{3,2,1,0:T(8,128)} reshape(f32[16,32768]{1,0:T(8,128)} %reduce.3) | data formatting | bytes 4194304
  83.7 2.8 copy.60
  86.5 2.3 bitcast_multiply_fusion
  88.8 5.0 %copy.61 = f32[128,8,8,64]{0,2,3,1:T(8,128)} copy(f32[128,8,8,64]{3,2,1,0:T(8,128)} %bitcast_multiply_fusion) | data formatting | bytes 4194304
  93.9 182.8 %while.16 = (s32[]{:T(128)}, f32[8,128,64]{1,2,0:T(8,128)S(1)}, f32[8,128,64]{1,2,0:T(8,128)S(1)}, f32[8,8,8,8,64]{2,3,4,1,0:T(8,128)}, s32[8]{0:T(128)S(1)}, /*...) while((s32[]{:T(128)}, f32[8,128,64]{1,2,0:T(8,128)S(1)}, ...), condition=%wide.region_5.6_spmd.clone.clone, body=%wide.region_2.5_spmd.clone.clone.sunk | while | flops 53850804 | bytes 15474387 | solution.py:141
  94.1 0.6 dynamic_slice.13
  95.2 18.6 %conditional.4 = (f32[8,128,64]{1,2,0:T(8,128)S(1)}, f32[8,128,64]{1,2,0:T(8,128)S(1)}, f32[1,8,8,8,64]{2,3,4,1,0:T(8,128)}) conditional(s32[]{:T(128)} %convert_element_type.412, (f32[8,128,64]{1,2,0:T(8,128)S(1)}, f32[8,128,64]{1,2,0:T(8,128)S(1)}) %tuple.139, (s32[]{:T(128)}, s32[8]{0:T(128)S(1)}, s32[8,1,1]{0,2,1:T(1,128)S(1)}, ...), branch_computations={%region_3.3_spmd, %region_4.4_spmd.clone} | conditional | flops 53850800 | bytes 11276004 | solution.py:136
  97.1 3.6 %fusion.11 = (f32[8,128,64]{1,2,0:T(8,128)S(1)}, f32[8,128,64]{1,2,0:T(8,128)S(1)}, f32[8,128,64]{1,2,0:T(8,128)S(1)}, f32[8,128,64]{1,2,0:T(8,128)S(1)}, f32[8,...) fusion(f32[128]{0:T(128)S(1)} %get-tuple-element.437, ...), kind=kLoop, calls=%fused_computation.9 | loop fusion | flops 3473408 | bytes 2684416 | tf_op jit(solution)/shard_map/while/body/eval_jaxpr/cond/branch_1_fun/jit(_where)/select_n | solution.py:91
  100.7 6.2 %stack.51 = f32[8,8,128,64]{2,0,3,1:T(8,128)} concatenate(f32[1,8,128,64]{2,0,3,1:T(1,128)} %bitcast.229, f32[1,8,128,64]{2,0,3,1:T(1,128)} %bitcast.228, f32[1,8,128,64]{2,0,3,1:T(1,128)} %bitcast.227, f32[1,8,128,64]{2,0,3,1:T(1,128)S(1)} %bitcast.226, f32[1,8,128,64]{2,0,3,1:T(1,128)S(1)} %bitcast.225, f32[1,8,128,64]{2,0,3,1:T(1,128)S(1)} %bitcast.224, ...), dimensions={0} | concatenate | bytes 4194304 | tf_op jit(solution)/shard_map/while/body/eval_jaxpr/cond/branch_1_fun/stack | solution.py:126
  106.9 6.9 %convolution_bitcast_fusion = f32[1,8,8,8,64]{2,3,4,1,0:T(8,128)} fusion(f32[8,8,128,64]{2,0,3,1:T(8,128)} %stack.51, f32[128,8,8,64]{0,2,3,1:T(8,128)} %get-tuple-element.428), kind=kOutput, calls=%fused_computation.4 | convolution fusion | flops 50331648 | bytes 4325376 | tf_op jit(solution)/shard_map/while/body/eval_jaxpr/cond/branch_1_fun/jgkq,kgcq->gcjq/dot_general | solution.py:127
  113.8 3.1 constant_dynamic-update-slice_fusion.2
  116.9 0.5 dynamic_slice.13
  118.1 18.6 %conditional.4 = (f32[8,128,64]{1,2,0:T(8,128)S(1)}, f32[8,128,64]{1,2,0:T(8,128)S(1)}, f32[1,8,8,8,64]{2,3,4,1,0:T(8,128)}) conditional(s32[]{:T(128)} %convert_element_type.412, (f32[8,128,64]{1,2,0:T(8,128)S(1)}, f32[8,128,64]{1,2,0:T(8,128)S(1)}) %tuple.139, (s32[]{:T(128)}, s32[8]{0:T(128)S(1)}, s32[8,1,1]{0,2,1:T(1,128)S(1)}, ...), branch_computations={%region_3.3_spmd, %region_4.4_spmd.clone} | conditional | flops 53850800 | bytes 11276004 | solution.py:136
  119.9 3.6 %fusion.11 = (f32[8,128,64]{1,2,0:T(8,128)S(1)}, f32[8,128,64]{1,2,0:T(8,128)S(1)}, f32[8,128,64]{1,2,0:T(8,128)S(1)}, f32[8,128,64]{1,2,0:T(8,128)S(1)}, f32[8,...) fusion(f32[128]{0:T(128)S(1)} %get-tuple-element.437, ...), kind=kLoop, calls=%fused_computation.9 | loop fusion | flops 3473408 | bytes 2684416 | tf_op jit(solution)/shard_map/while/body/eval_jaxpr/cond/branch_1_fun/jit(_where)/select_n | solution.py:91
  123.5 6.2 %stack.51 = f32[8,8,128,64]{2,0,3,1:T(8,128)} concatenate(f32[1,8,128,64]{2,0,3,1:T(1,128)} %bitcast.229, f32[1,8,128,64]{2,0,3,1:T(1,128)} %bitcast.228, f32[1,8,128,64]{2,0,3,1:T(1,128)} %bitcast.227, f32[1,8,128,64]{2,0,3,1:T(1,128)S(1)} %bitcast.226, f32[1,8,128,64]{2,0,3,1:T(1,128)S(1)} %bitcast.225, f32[1,8,128,64]{2,0,3,1:T(1,128)S(1)} %bitcast.224, ...), dimensions={0} | concatenate | bytes 4194304 | tf_op jit(solution)/shard_map/while/body/eval_jaxpr/cond/branch_1_fun/stack | solution.py:126
  129.7 6.9 %convolution_bitcast_fusion = f32[1,8,8,8,64]{2,3,4,1,0:T(8,128)} fusion(f32[8,8,128,64]{2,0,3,1:T(8,128)} %stack.51, f32[128,8,8,64]{0,2,3,1:T(8,128)} %get-tuple-element.428), kind=kOutput, calls=%fused_computation.4 | convolution fusion | flops 50331648 | bytes 4325376 | tf_op jit(solution)/shard_map/while/body/eval_jaxpr/cond/branch_1_fun/jgkq,kgcq->gcjq/dot_general | solution.py:127
  136.7 3.1 constant_dynamic-update-slice_fusion.2
  139.7 0.5 dynamic_slice.13
  140.9 18.6 %conditional.4 = (f32[8,128,64]{1,2,0:T(8,128)S(1)}, f32[8,128,64]{1,2,0:T(8,128)S(1)}, f32[1,8,8,8,64]{2,3,4,1,0:T(8,128)}) conditional(s32[]{:T(128)} %convert_element_type.412, (f32[8,128,64]{1,2,0:T(8,128)S(1)}, f32[8,128,64]{1,2,0:T(8,128)S(1)}) %tuple.139, (s32[]{:T(128)}, s32[8]{0:T(128)S(1)}, s32[8,1,1]{0,2,1:T(1,128)S(1)}, ...), branch_computations={%region_3.3_spmd, %region_4.4_spmd.clone} | conditional | flops 53850800 | bytes 11276004 | solution.py:136
  142.7 3.6 %fusion.11 = (f32[8,128,64]{1,2,0:T(8,128)S(1)}, f32[8,128,64]{1,2,0:T(8,128)S(1)}, f32[8,128,64]{1,2,0:T(8,128)S(1)}, f32[8,128,64]{1,2,0:T(8,128)S(1)}, f32[8,...) fusion(f32[128]{0:T(128)S(1)} %get-tuple-element.437, ...), kind=kLoop, calls=%fused_computation.9 | loop fusion | flops 3473408 | bytes 2684416 | tf_op jit(solution)/shard_map/while/body/eval_jaxpr/cond/branch_1_fun/jit(_where)/select_n | solution.py:91
  146.3 6.2 %stack.51 = f32[8,8,128,64]{2,0,3,1:T(8,128)} concatenate(f32[1,8,128,64]{2,0,3,1:T(1,128)} %bitcast.229, f32[1,8,128,64]{2,0,3,1:T(1,128)} %bitcast.228, f32[1,8,128,64]{2,0,3,1:T(1,128)} %bitcast.227, f32[1,8,128,64]{2,0,3,1:T(1,128)S(1)} %bitcast.226, f32[1,8,128,64]{2,0,3,1:T(1,128)S(1)} %bitcast.225, f32[1,8,128,64]{2,0,3,1:T(1,128)S(1)} %bitcast.224, ...), dimensions={0} | concatenate | bytes 4194304 | tf_op jit(solution)/shard_map/while/body/eval_jaxpr/cond/branch_1_fun/stack | solution.py:126
  152.5 6.9 %convolution_bitcast_fusion = f32[1,8,8,8,64]{2,3,4,1,0:T(8,128)} fusion(f32[8,8,128,64]{2,0,3,1:T(8,128)} %stack.51, f32[128,8,8,64]{0,2,3,1:T(8,128)} %get-tuple-element.428), kind=kOutput, calls=%fused_computation.4 | convolution fusion | flops 50331648 | bytes 4325376 | tf_op jit(solution)/shard_map/while/body/eval_jaxpr/cond/branch_1_fun/jgkq,kgcq->gcjq/dot_general | solution.py:127
  159.5 3.1 constant_dynamic-update-slice_fusion.2
  163.7 18.6 %conditional.4 = (f32[8,128,64]{1,2,0:T(8,128)S(1)}, f32[8,128,64]{1,2,0:T(8,128)S(1)}, f32[1,8,8,8,64]{2,3,4,1,0:T(8,128)}) conditional(s32[]{:T(128)} %convert_element_type.412, (f32[8,128,64]{1,2,0:T(8,128)S(1)}, f32[8,128,64]{1,2,0:T(8,128)S(1)}) %tuple.139, (s32[]{:T(128)}, s32[8]{0:T(128)S(1)}, s32[8,1,1]{0,2,1:T(1,128)S(1)}, ...), branch_computations={%region_3.3_spmd, %region_4.4_spmd.clone} | conditional | flops 53850800 | bytes 11276004 | solution.py:136
  165.5 3.6 %fusion.11 = (f32[8,128,64]{1,2,0:T(8,128)S(1)}, f32[8,128,64]{1,2,0:T(8,128)S(1)}, f32[8,128,64]{1,2,0:T(8,128)S(1)}, f32[8,128,64]{1,2,0:T(8,128)S(1)}, f32[8,...) fusion(f32[128]{0:T(128)S(1)} %get-tuple-element.437, ...), kind=kLoop, calls=%fused_computation.9 | loop fusion | flops 3473408 | bytes 2684416 | tf_op jit(solution)/shard_map/while/body/eval_jaxpr/cond/branch_1_fun/jit(_where)/select_n | solution.py:91
  169.1 6.2 %stack.51 = f32[8,8,128,64]{2,0,3,1:T(8,128)} concatenate(f32[1,8,128,64]{2,0,3,1:T(1,128)} %bitcast.229, f32[1,8,128,64]{2,0,3,1:T(1,128)} %bitcast.228, f32[1,8,128,64]{2,0,3,1:T(1,128)} %bitcast.227, f32[1,8,128,64]{2,0,3,1:T(1,128)S(1)} %bitcast.226, f32[1,8,128,64]{2,0,3,1:T(1,128)S(1)} %bitcast.225, f32[1,8,128,64]{2,0,3,1:T(1,128)S(1)} %bitcast.224, ...), dimensions={0} | concatenate | bytes 4194304 | tf_op jit(solution)/shard_map/while/body/eval_jaxpr/cond/branch_1_fun/stack | solution.py:126
  175.3 6.9 %convolution_bitcast_fusion = f32[1,8,8,8,64]{2,3,4,1,0:T(8,128)} fusion(f32[8,8,128,64]{2,0,3,1:T(8,128)} %stack.51, f32[128,8,8,64]{0,2,3,1:T(8,128)} %get-tuple-element.428), kind=kOutput, calls=%fused_computation.4 | convolution fusion | flops 50331648 | bytes 4325376 | tf_op jit(solution)/shard_map/while/body/eval_jaxpr/cond/branch_1_fun/jgkq,kgcq->gcjq/dot_general | solution.py:127
  182.3 3.1 constant_dynamic-update-slice_fusion.2
  186.5 18.6 %conditional.4 = (f32[8,128,64]{1,2,0:T(8,128)S(1)}, f32[8,128,64]{1,2,0:T(8,128)S(1)}, f32[1,8,8,8,64]{2,3,4,1,0:T(8,128)}) conditional(s32[]{:T(128)} %convert_element_type.412, (f32[8,128,64]{1,2,0:T(8,128)S(1)}, f32[8,128,64]{1,2,0:T(8,128)S(1)}) %tuple.139, (s32[]{:T(128)}, s32[8]{0:T(128)S(1)}, s32[8,1,1]{0,2,1:T(1,128)S(1)}, ...), branch_computations={%region_3.3_spmd, %region_4.4_spmd.clone} | conditional | flops 53850800 | bytes 11276004 | solution.py:136
  188.4 3.6 %fusion.11 = (f32[8,128,64]{1,2,0:T(8,128)S(1)}, f32[8,128,64]{1,2,0:T(8,128)S(1)}, f32[8,128,64]{1,2,0:T(8,128)S(1)}, f32[8,128,64]{1,2,0:T(8,128)S(1)}, f32[8,...) fusion(f32[128]{0:T(128)S(1)} %get-tuple-element.437, ...), kind=kLoop, calls=%fused_computation.9 | loop fusion | flops 3473408 | bytes 2684416 | tf_op jit(solution)/shard_map/while/body/eval_jaxpr/cond/branch_1_fun/jit(_where)/select_n | solution.py:91
  191.9 6.2 %stack.51 = f32[8,8,128,64]{2,0,3,1:T(8,128)} concatenate(f32[1,8,128,64]{2,0,3,1:T(1,128)} %bitcast.229, f32[1,8,128,64]{2,0,3,1:T(1,128)} %bitcast.228, f32[1,8,128,64]{2,0,3,1:T(1,128)} %bitcast.227, f32[1,8,128,64]{2,0,3,1:T(1,128)S(1)} %bitcast.226, f32[1,8,128,64]{2,0,3,1:T(1,128)S(1)} %bitcast.225, f32[1,8,128,64]{2,0,3,1:T(1,128)S(1)} %bitcast.224, ...), dimensions={0} | concatenate | bytes 4194304 | tf_op jit(solution)/shard_map/while/body/eval_jaxpr/cond/branch_1_fun/stack | solution.py:126
  198.2 6.9 %convolution_bitcast_fusion = f32[1,8,8,8,64]{2,3,4,1,0:T(8,128)} fusion(f32[8,8,128,64]{2,0,3,1:T(8,128)} %stack.51, f32[128,8,8,64]{0,2,3,1:T(8,128)} %get-tuple-element.428), kind=kOutput, calls=%fused_computation.4 | convolution fusion | flops 50331648 | bytes 4325376 | tf_op jit(solution)/shard_map/while/body/eval_jaxpr/cond/branch_1_fun/jgkq,kgcq->gcjq/dot_general | solution.py:127
  205.1 3.1 constant_dynamic-update-slice_fusion.2
  209.4 18.6 %conditional.4 = (f32[8,128,64]{1,2,0:T(8,128)S(1)}, f32[8,128,64]{1,2,0:T(8,128)S(1)}, f32[1,8,8,8,64]{2,3,4,1,0:T(8,128)}) conditional(s32[]{:T(128)} %convert_element_type.412, (f32[8,128,64]{1,2,0:T(8,128)S(1)}, f32[8,128,64]{1,2,0:T(8,128)S(1)}) %tuple.139, (s32[]{:T(128)}, s32[8]{0:T(128)S(1)}, s32[8,1,1]{0,2,1:T(1,128)S(1)}, ...), branch_computations={%region_3.3_spmd, %region_4.4_spmd.clone} | conditional | flops 53850800 | bytes 11276004 | solution.py:136
  211.2 3.6 %fusion.11 = (f32[8,128,64]{1,2,0:T(8,128)S(1)}, f32[8,128,64]{1,2,0:T(8,128)S(1)}, f32[8,128,64]{1,2,0:T(8,128)S(1)}, f32[8,128,64]{1,2,0:T(8,128)S(1)}, f32[8,...) fusion(f32[128]{0:T(128)S(1)} %get-tuple-element.437, ...), kind=kLoop, calls=%fused_computation.9 | loop fusion | flops 3473408 | bytes 2684416 | tf_op jit(solution)/shard_map/while/body/eval_jaxpr/cond/branch_1_fun/jit(_where)/select_n | solution.py:91
  214.8 6.2 %stack.51 = f32[8,8,128,64]{2,0,3,1:T(8,128)} concatenate(f32[1,8,128,64]{2,0,3,1:T(1,128)} %bitcast.229, f32[1,8,128,64]{2,0,3,1:T(1,128)} %bitcast.228, f32[1,8,128,64]{2,0,3,1:T(1,128)} %bitcast.227, f32[1,8,128,64]{2,0,3,1:T(1,128)S(1)} %bitcast.226, f32[1,8,128,64]{2,0,3,1:T(1,128)S(1)} %bitcast.225, f32[1,8,128,64]{2,0,3,1:T(1,128)S(1)} %bitcast.224, ...), dimensions={0} | concatenate | bytes 4194304 | tf_op jit(solution)/shard_map/while/body/eval_jaxpr/cond/branch_1_fun/stack | solution.py:126
  221.0 6.9 %convolution_bitcast_fusion = f32[1,8,8,8,64]{2,3,4,1,0:T(8,128)} fusion(f32[8,8,128,64]{2,0,3,1:T(8,128)} %stack.51, f32[128,8,8,64]{0,2,3,1:T(8,128)} %get-tuple-element.428), kind=kOutput, calls=%fused_computation.4 | convolution fusion | flops 50331648 | bytes 4325376 | tf_op jit(solution)/shard_map/while/body/eval_jaxpr/cond/branch_1_fun/jgkq,kgcq->gcjq/dot_general | solution.py:127
  228.0 3.1 constant_dynamic-update-slice_fusion.2
  232.2 18.6 %conditional.4 = (f32[8,128,64]{1,2,0:T(8,128)S(1)}, f32[8,128,64]{1,2,0:T(8,128)S(1)}, f32[1,8,8,8,64]{2,3,4,1,0:T(8,128)}) conditional(s32[]{:T(128)} %convert_element_type.412, (f32[8,128,64]{1,2,0:T(8,128)S(1)}, f32[8,128,64]{1,2,0:T(8,128)S(1)}) %tuple.139, (s32[]{:T(128)}, s32[8]{0:T(128)S(1)}, s32[8,1,1]{0,2,1:T(1,128)S(1)}, ...), branch_computations={%region_3.3_spmd, %region_4.4_spmd.clone} | conditional | flops 53850800 | bytes 11276004 | solution.py:136
  234.0 3.6 %fusion.11 = (f32[8,128,64]{1,2,0:T(8,128)S(1)}, f32[8,128,64]{1,2,0:T(8,128)S(1)}, f32[8,128,64]{1,2,0:T(8,128)S(1)}, f32[8,128,64]{1,2,0:T(8,128)S(1)}, f32[8,...) fusion(f32[128]{0:T(128)S(1)} %get-tuple-element.437, ...), kind=kLoop, calls=%fused_computation.9 | loop fusion | flops 3473408 | bytes 2684416 | tf_op jit(solution)/shard_map/while/body/eval_jaxpr/cond/branch_1_fun/jit(_where)/select_n | solution.py:91
  237.6 6.2 %stack.51 = f32[8,8,128,64]{2,0,3,1:T(8,128)} concatenate(f32[1,8,128,64]{2,0,3,1:T(1,128)} %bitcast.229, f32[1,8,128,64]{2,0,3,1:T(1,128)} %bitcast.228, f32[1,8,128,64]{2,0,3,1:T(1,128)} %bitcast.227, f32[1,8,128,64]{2,0,3,1:T(1,128)S(1)} %bitcast.226, f32[1,8,128,64]{2,0,3,1:T(1,128)S(1)} %bitcast.225, f32[1,8,128,64]{2,0,3,1:T(1,128)S(1)} %bitcast.224, ...), dimensions={0} | concatenate | bytes 4194304 | tf_op jit(solution)/shard_map/while/body/eval_jaxpr/cond/branch_1_fun/stack | solution.py:126
  243.8 6.9 %convolution_bitcast_fusion = f32[1,8,8,8,64]{2,3,4,1,0:T(8,128)} fusion(f32[8,8,128,64]{2,0,3,1:T(8,128)} %stack.51, f32[128,8,8,64]{0,2,3,1:T(8,128)} %get-tuple-element.428), kind=kOutput, calls=%fused_computation.4 | convolution fusion | flops 50331648 | bytes 4325376 | tf_op jit(solution)/shard_map/while/body/eval_jaxpr/cond/branch_1_fun/jgkq,kgcq->gcjq/dot_general | solution.py:127
  250.8 3.1 constant_dynamic-update-slice_fusion.2
  255.0 18.6 %conditional.4 = (f32[8,128,64]{1,2,0:T(8,128)S(1)}, f32[8,128,64]{1,2,0:T(8,128)S(1)}, f32[1,8,8,8,64]{2,3,4,1,0:T(8,128)}) conditional(s32[]{:T(128)} %convert_element_type.412, (f32[8,128,64]{1,2,0:T(8,128)S(1)}, f32[8,128,64]{1,2,0:T(8,128)S(1)}) %tuple.139, (s32[]{:T(128)}, s32[8]{0:T(128)S(1)}, s32[8,1,1]{0,2,1:T(1,128)S(1)}, ...), branch_computations={%region_3.3_spmd, %region_4.4_spmd.clone} | conditional | flops 53850800 | bytes 11276004 | solution.py:136
  256.8 3.6 %fusion.11 = (f32[8,128,64]{1,2,0:T(8,128)S(1)}, f32[8,128,64]{1,2,0:T(8,128)S(1)}, f32[8,128,64]{1,2,0:T(8,128)S(1)}, f32[8,128,64]{1,2,0:T(8,128)S(1)}, f32[8,...) fusion(f32[128]{0:T(128)S(1)} %get-tuple-element.437, ...), kind=kLoop, calls=%fused_computation.9 | loop fusion | flops 3473408 | bytes 2684416 | tf_op jit(solution)/shard_map/while/body/eval_jaxpr/cond/branch_1_fun/jit(_where)/select_n | solution.py:91
  260.4 6.2 %stack.51 = f32[8,8,128,64]{2,0,3,1:T(8,128)} concatenate(f32[1,8,128,64]{2,0,3,1:T(1,128)} %bitcast.229, f32[1,8,128,64]{2,0,3,1:T(1,128)} %bitcast.228, f32[1,8,128,64]{2,0,3,1:T(1,128)} %bitcast.227, f32[1,8,128,64]{2,0,3,1:T(1,128)S(1)} %bitcast.226, f32[1,8,128,64]{2,0,3,1:T(1,128)S(1)} %bitcast.225, f32[1,8,128,64]{2,0,3,1:T(1,128)S(1)} %bitcast.224, ...), dimensions={0} | concatenate | bytes 4194304 | tf_op jit(solution)/shard_map/while/body/eval_jaxpr/cond/branch_1_fun/stack | solution.py:126
  266.7 6.9 %convolution_bitcast_fusion = f32[1,8,8,8,64]{2,3,4,1,0:T(8,128)} fusion(f32[8,8,128,64]{2,0,3,1:T(8,128)} %stack.51, f32[128,8,8,64]{0,2,3,1:T(8,128)} %get-tuple-element.428), kind=kOutput, calls=%fused_computation.4 | convolution fusion | flops 50331648 | bytes 4325376 | tf_op jit(solution)/shard_map/while/body/eval_jaxpr/cond/branch_1_fun/jgkq,kgcq->gcjq/dot_general | solution.py:127
  273.6 3.0 constant_dynamic-update-slice_fusion.2
  276.7 11.1 %copy.62 = f32[8,8,8,8,64]{4,3,2,1,0:T(8,128)} copy(f32[8,8,8,8,64]{1,3,4,0,2:T(8,128)} %bitcast.221) | data formatting | bytes 2097152 | tf_op jit(solution)/shard_map/transpose | solution.py:144
  287.8 8.5 %multiply_reduce_fusion = f32[8,8,8]{0,2,1:T(8,128)S(1)} fusion(f32[64]{0:T(128)S(1)} %compare_select_fusion.9, f32[8,8]{1,0:T(8,128)S(1)} %sqrt_multiply_fusion, f32[8,8,8,8,64]{2,3,4,1,0:T(8,128)} %get-tuple-element.216), kind=kLoop, calls=%fused_computation.97 | loop fusion | flops 1048064 | bytes 1051136 | tf_op jit(solution)/shard_map/reduce_sum | solution.py:152
  296.5 45.8 %psum.7 = f32[4,64]{1,0:T(4,128)} all-reduce(f32[4,64]{1,0:T(4,128)S(1)} %broadcast_divide_fusion), channel_id=1, replica_groups=mesh['beta'=16,'grp'=2] {'beta'}, use_global_device_ids=true, to_apply=%region_8.9 | all-reduce | flops 256 | bytes 2048 | tf_op jit(solution)/shard_map/psum | solution.py:179
  342.3 3.3 broadcast_multiply_fusion
  (264 shorter events, 12.5 us)
Async XLA Ops:
  0.6 1.6 copy-start
  18.8 51.5 %all-to-all-start = ((f32[16,1,32768]{2,1,0:T(1,128)}), f32[16,1,32768]{2,1,0:T(1,128)}, u32[]{:S(2)}, u32[]{:S(2)}) async-start(f32[16,1,32768]{2,1,0:T(1,128)} %reshape.2457), calls=%async_computation | async-start | bytes 4194304 | tf_op jit(solution)/shard_map/all_to_all | solution.py:173
  94.1 1.1 copy-start.2
  113.8 3.1 copy-start.3
  116.9 1.1 copy-start.2
  136.7 3.1 copy-start.3
  139.7 1.1 copy-start.2
  159.5 3.1 copy-start.3
  162.6 1.1 copy-start.2
  182.3 3.1 copy-start.3
  185.4 1.1 copy-start.2
  205.1 3.1 copy-start.3
  208.3 1.1 copy-start.2
  228.0 3.1 copy-start.3
  231.1 1.1 copy-start.2
  250.8 3.1 copy-start.3
  253.9 1.1 copy-start.2
  273.6 3.0 copy-start.3
  287.8 8.7 %copy-start.1 = (f32[64]{0:T(128)S(1)}, f32[64]{0:T(128)}, u32[]{:S(2)}) copy-start(f32[64]{0:T(128)} %fusion.87) | copy-start | bytes 772
where the time goes:
time: 351 us; the launch traced here: 346 us
  local copies, waits for them, and re-layouts  117 us (33%)
  other arithmetic  62.1 us (18%)
  matrix products  59.5 us (17%)
  blocking collectives  45.8 us (13%)
  waiting for transfers between devices  38.1 us (11%)
  loops' own time  11.6 us (3%)
  starting transfers between devices  8.4 us (2%)
  between operations  3.57 us (1%)
    dot_general x8, matrix products, compute_block(): jnp.einsum('jgkq,kgcq->gcjq', stacked, weighted, precision=HIGHEST)  55.6 us
    another operation x8, local copies, waits for them, and re-layouts, compute_block(): stacked = jnp.stack(levels, axis=0)  49.9 us
    psum x1, blocking collectives, local(): power = lax.psum(power_part, 'beta')  45.8 us
    all_to_all x1, waiting for transfers between devices, local(): lax.all_to_all(spectrum, 'beta', split_axis=1, concat_axis=0, tiled=True)  38.1 us
    select_n x8, other arithmetic, advance(): renewed = jnp.where(degree == lowest, start_value, recurred)  28.7 us
    dynamic_update_slice x8, local copies, waits for them, and re-layouts, degree_rows(): lax.scan(block_step, (empty_state, empty_state), jnp.arange(block_count,...  24.7 us
    unnamed x7, local copies, waits for them, and re-layouts  15.6 us
    transpose x1, local copies, waits for them, and re-layouts, degree_rows(): jnp.transpose(parts, (1, 2, 0, 3, 4))  11.1 us
  transfers between devices with their start and end apart: 1, of which 1 were waited for; matrix products, arithmetic and copies ran while one was open for 1% of the time, Pallas kernels for 0%

commit v1 on v0

--- a/solution.py
+++ b/solution.py
@@ -1,9 +1,16 @@
+import math
+
 import jax
 import jax.numpy as jnp
+import numpy as np
 from jax import lax
+from jax.experimental import pallas as pl
+from jax.experimental.pallas import tpu as pltpu
 from jax.sharding import PartitionSpec as P
 
 HIGHEST = lax.Precision.HIGHEST
+SUBLANES = 8
+LANES = 128
 
 
 def beta_angles(spread):
@@ -154,7 +161,7 @@
     return energy_sum / (degrees * degrees)[None, :]
 
 
-def local(samples):
+def general_local(samples):
     devices = lax.axis_size("beta")
     device = lax.axis_index("beta")
     local_beta = samples.shape[0]
@@ -181,6 +188,243 @@
     return (coeffs, power)
 
 
+def wigner_quarter(spread):
+    alpha = np.arange(1 - spread, spread)[:, None]
+    gamma = np.arange(spread)[None, :]
+    lowest = np.maximum(np.abs(alpha), gamma)
+    shift = np.maximum(0, gamma - alpha)
+    logs = np.array([math.lgamma(value + 1.0) for value in range(2 * spread)])
+    magnitude = 0.5 * (
+        logs[lowest + alpha] + logs[lowest - alpha] + logs[lowest + gamma] + logs[lowest - gamma]
+    )
+    magnitude = magnitude - logs[lowest + gamma - shift] - logs[shift]
+    magnitude = magnitude - logs[alpha - gamma + shift] - logs[lowest - alpha - shift]
+    sign = 1.0 - 2.0 * ((alpha - gamma + shift) % 2)
+    first = sign * np.exp(magnitude - lowest * math.log(2.0))
+    squares_a, squares_g = alpha.astype(np.float64) ** 2, gamma.astype(np.float64) ** 2
+    former, current, levels = np.zeros(first.shape), np.zeros(first.shape), []
+    for degree in range(spread):
+        before = degree - 1.0
+        upper = np.sqrt(np.maximum((degree**2 - squares_a) * (degree**2 - squares_g), 1.0))
+        lower = np.sqrt(np.maximum((before**2 - squares_a) * (before**2 - squares_g), 0.0))
+        cross = alpha * gamma / max(before * degree, 1.0)
+        follow = degree * (2.0 * before + 1.0) / upper * -cross * current
+        follow = follow - degree * lower / (max(before, 1.0) * upper) * former
+        former, current = current, np.where(lowest == degree, first, follow)
+        levels.append(current)
+    return np.stack(levels)
+
+
+def split_pair(table):
+    high = np.asarray(table).astype(jnp.bfloat16)
+    return high, (table - high.astype(np.float64)).astype(jnp.bfloat16)
+
+
+def fourier_tables(spread):
+    grid = 2 * spread
+    at = np.arange(grid)
+    phase = 2.0 * np.pi / grid * (at[:, None] * np.arange(spread)[None, :] % grid)
+    cosine, sine = np.cos(phase), -np.sin(phase)
+    gamma_part = np.concatenate([cosine, sine, sine, -cosine], axis=1)
+    phase = 2.0 * np.pi / grid * (at[:, None] * at[None, :] % grid)
+    alpha_part = np.concatenate([np.cos(phase), np.sin(phase)], axis=1) / grid
+    return gamma_part, alpha_part
+
+
+def beta_table(spread):
+    angles = (2.0 * np.arange(2 * spread) + 1.0) * (np.pi / (4.0 * spread))
+    odd = 2.0 * np.arange(spread) + 1.0
+    series = np.sum(np.sin(angles[:, None] * odd[None, :]) / odd[None, :], axis=1)
+    weight = 2.0 / spread * np.sin(angles) * series
+    order = np.arange(spread)
+    fold = np.where(order == 0, 1.0, 2.0)[:, None] * weight[None, :]
+    turn = order[:, None] * angles[None, :]
+    return np.concatenate([fold * np.cos(turn), fold * np.sin(turn)], axis=1)
+
+
+def sign_masks(spread):
+    step = (np.arange(SUBLANES)[:, None] - np.arange(spread)[None, :]) % 4
+    even = np.where(step == 0, 1.0, np.where(step == 2, -1.0, 0.0))
+    odd = np.where(step == 3, 1.0, np.where(step == 1, -1.0, 0.0))
+    return np.concatenate([even, even], axis=1), np.concatenate([odd, odd], axis=1)
+
+
+def block_steps(spread):
+    width = LANES // SUBLANES
+    return [
+        (block, chunk)
+        for block in range(spread // SUBLANES)
+        for chunk in range(-(-(block + 1) * SUBLANES // width))
+    ]
+
+
+def quarter_tables(spread, devices):
+    quarter = wigner_quarter(spread)
+    grid, width = 2 * spread, LANES // SUBLANES
+    rows = np.arange(grid)
+    orders = np.where(rows < spread, rows, rows - grid)
+    held = np.clip(orders + spread - 1, 0, 2 * spread - 2)
+    by_row = np.where((orders > -spread)[None, :, None], quarter[:, held, :], 0.0)
+    by_row = by_row * (8.0 * np.sqrt(2.0 * np.arange(spread) + 1.0))[:, None, None]
+    gammas, alphas = [], []
+    for block, chunk in block_steps(spread):
+        degrees = slice(block * SUBLANES, (block + 1) * SUBLANES)
+        part = slice(chunk * width, (chunk + 1) * width)
+        table = np.swapaxes(quarter[degrees, spread - 1 :, part], 1, 2).reshape(LANES, spread)
+        gammas.append(np.concatenate([table, table], axis=1))
+        table = np.swapaxes(by_row[degrees, :, part], 0, 1).reshape(devices, SUBLANES, LANES)
+        alphas.append(table)
+    return np.stack(gammas).astype(np.float32), np.stack(alphas, axis=1).astype(np.float32)
+
+
+def split_value(value):
+    high = value.astype(jnp.bfloat16)
+    return high, (value - high.astype(jnp.float32)).astype(jnp.bfloat16)
+
+
+def dot(left, right):
+    return jnp.dot(left, right, preferred_element_type=jnp.float32)
+
+
+def spectrum_kernel(x_ref, gamma_hi, gamma_lo, alpha_hi, alpha_lo, out_ref):
+    count, _, grid, _ = x_ref.shape
+    blocks = out_ref.shape[0]
+    for k in range(count):
+        high, low = split_value(x_ref[k, 0])
+        half = dot(high, gamma_hi[...]) + dot(low, gamma_hi[...]) + dot(high, gamma_lo[...])
+        pair = jnp.concatenate([half[:, :LANES], half[:, LANES:]], axis=0)
+        high, low = split_value(pair)
+        rows = dot(alpha_hi[...], high) + dot(alpha_lo[...], high) + dot(alpha_hi[...], low)
+        for d in range(blocks):
+            out_ref[d, 0, pl.ds(k, SUBLANES, stride=count), :] = rows[
+                d * SUBLANES : (d + 1) * SUBLANES
+            ]
+
+
+def spectrum_call(samples, devices):
+    count, functions, grid, _ = samples.shape
+    gamma_part, alpha_part = fourier_tables(grid // 2)
+    tables = [*split_pair(gamma_part), *split_pair(alpha_part)]
+    rows = grid // devices * count
+    whole = lambda table: pl.BlockSpec(table.shape, lambda f: (0, 0))
+    return pl.pallas_call(
+        spectrum_kernel,
+        grid=(functions,),
+        in_specs=[pl.BlockSpec((count, 1, grid, grid), lambda f: (0, f, 0, 0))]
+        + [whole(table) for table in tables],
+        out_specs=pl.BlockSpec((devices, 1, rows, LANES), lambda f: (0, f, 0, 0)),
+        out_shape=jax.ShapeDtypeStruct((devices, functions, rows, LANES), jnp.float32),
+        name="spectrum",
+    )(samples, *tables)
+
+
+def degree_kernel(
+    r_ref, beta_hi, beta_lo, even_ref, odd_ref, gamma_ref, alpha_ref, out_ref, pow_ref, t_ref, c_ref
+):
+    sources, functions, held, _ = r_ref.shape
+    count = held // SUBLANES
+    spread = beta_hi.shape[0]
+    width = LANES // SUBLANES
+    for f in range(0, functions, 2):
+        for n in range(SUBLANES):
+            parts = [
+                r_ref[:, f + i, n * count : (n + 1) * count, :].reshape(sources * count, LANES)
+                for i in range(2)
+            ]
+            high, low = split_value(jnp.concatenate(parts, axis=1))
+            even = jnp.concatenate([even_ref[n : n + 1, :]] * 2, axis=1)
+            odd = jnp.concatenate([odd_ref[n : n + 1, :]] * 2, axis=1)
+            high = jnp.concatenate([high * even, high * odd], axis=0)
+            low = jnp.concatenate([low * even, low * odd], axis=0)
+            turned = dot(beta_hi[...], high) + dot(beta_lo[...], high) + dot(beta_hi[...], low)
+            for i in range(2):
+                for b in range(spread // SUBLANES):
+                    t_ref[f + i, pl.ds(b * SUBLANES * SUBLANES + n, SUBLANES, stride=SUBLANES), :] = (
+                        turned[b * SUBLANES : (b + 1) * SUBLANES, i * LANES : (i + 1) * LANES]
+                    )
+
+    lane = lax.broadcasted_iota(jnp.int32, (SUBLANES, LANES), 1)
+    fold = jnp.where(lane % spread == 0, 1.0, 2.0).astype(jnp.float32)
+
+    def block_step(block, first):
+        chunks = (block * SUBLANES + SUBLANES + width - 1) // width
+
+        def chunk_step(chunk, totals):
+            totals = list(totals)
+            column = alpha_ref[first + chunk]
+            for m in range(width):
+                row = pl.multiple_of((chunk * width + m) * SUBLANES, SUBLANES)
+                values = [t_ref[f, pl.ds(row, SUBLANES), :] for f in range(functions)]
+                for j in range(SUBLANES):
+                    at = j * width + m
+                    table = gamma_ref[first + chunk, pl.ds(at, SUBLANES, stride=0), :]
+                    factor = jnp.broadcast_to(column[:, at : at + 1], (SUBLANES, LANES)) * table
+                    for f in range(functions):
+                        totals[j * functions + f] += factor * values[f]
+            return tuple(totals)
+
+        zero = jnp.zeros((SUBLANES, LANES), jnp.float32)
+        totals = lax.fori_loop(0, chunks, chunk_step, (zero,) * (SUBLANES * functions))
+        degree = pl.multiple_of(block * SUBLANES, SUBLANES)
+        for f in range(functions):
+            for j in range(SUBLANES):
+                c_ref[f, pl.ds(j, SUBLANES, stride=SUBLANES), :] = totals[j * functions + f]
+            energy = zero
+            for n in range(SUBLANES):
+                tile = c_ref[f, n * SUBLANES : (n + 1) * SUBLANES, :]
+                energy += tile * tile
+                out_ref[n, 0, f, pl.ds(degree, SUBLANES), :] = tile[:, :spread]
+                out_ref[n, 1, f, pl.ds(degree, SUBLANES), :] = tile[:, spread:]
+            pow_ref[f, pl.ds(degree, SUBLANES), :] = energy * fold
+        return first + chunks
+
+    lax.fori_loop(0, spread // SUBLANES, block_step, 0)
+
+
+def degree_call(received, gammas, alphas, spread):
+    functions = received.shape[1]
+    tables = [*split_pair(beta_table(spread))]
+    tables += [mask.astype(jnp.bfloat16) for mask in sign_masks(spread)]
+    return pl.pallas_call(
+        degree_kernel,
+        out_shape=[
+            jax.ShapeDtypeStruct((SUBLANES, 2, functions, spread, spread), jnp.float32),
+            jax.ShapeDtypeStruct((functions, spread, LANES), jnp.float32),
+        ],
+        scratch_shapes=[
+            pltpu.VMEM((functions, spread * SUBLANES, LANES), jnp.float32),
+            pltpu.VMEM((functions, SUBLANES * SUBLANES, LANES), jnp.float32),
+        ],
+        name="degrees",
+    )(received, *tables, gammas, alphas)
+
+
+def fast_local(samples):
+    devices = lax.axis_size("beta")
+    device = lax.axis_index("beta")
+    functions, grid_size = samples.shape[1:3]
+    spread = grid_size // 2
+    sent = spectrum_call(samples, devices)
+    received = lax.all_to_all(sent, "beta", split_axis=0, concat_axis=0, tiled=True)
+    gammas, alphas = quarter_tables(spread, devices)
+    alphas = lax.dynamic_index_in_dim(jnp.asarray(alphas), device, 0, keepdims=False)
+    coeffs, energy = degree_call(received, jnp.asarray(gammas), alphas, spread)
+    share = jnp.sum(energy, axis=-1)
+    shares = jnp.broadcast_to(share[None], (devices, functions, spread))
+    shares = lax.all_to_all(shares, "beta", split_axis=0, concat_axis=0, tiled=True)
+    degrees = 2.0 * jnp.arange(spread, dtype=jnp.float32) + 1.0
+    return coeffs, jnp.sum(shares, axis=0) / (degrees * degrees)[None, :]
+
+
+def local(samples):
+    devices = lax.axis_size("beta")
+    local_beta, functions, grid_size = samples.shape[:3]
+    tiled = grid_size == LANES and local_beta == SUBLANES and grid_size == devices * SUBLANES
+    if tiled and functions % 2 == 0:
+        return fast_local(samples)
+    return general_local(samples)
+
+
 def solution(mesh):
     return jax.shard_map(
         local,

time: 351 us -> 93.2 us (0.27); the launches traced: 346 us -> 92.9 us
  local copies, waits for them, and re-layouts: 117 us -> 4.16 us
  other arithmetic: 62.1 us -> 2.32 us
  matrix products: 59.5 us -> 0 us
  blocking collectives: 45.8 us -> 0 us
  Pallas kernels: 0 us -> 18.5 us
  loops' own time: 11.6 us -> 0 us
  waiting for transfers between devices: 38.1 us -> 48.8 us
  starting transfers between devices: 8.4 us -> 18.3 us
    dot_general x10 -> x0, matrix products: 59.5 us -> none  [the longest x8 55.6 us: compute_block(): jnp.einsum('jgkq,kgcq->gcjq', stacked, weighted, precision=HIGHEST)]
    another operation x8 -> x0, local copies, waits for them, and re-layouts: 49.9 us -> none  [compute_block(): stacked = jnp.stack(levels, axis=0)]
    psum x1 -> x0, blocking collectives: 45.8 us -> none  [local(): power = lax.psum(power_part, 'beta')]
    select_n x9 -> x0, other arithmetic: 28.7 us -> none  [the longest x8 28.7 us: advance(): renewed = jnp.where(degree == lowest, start_value, recurred)]
    dynamic_update_slice x8 -> x0, local copies, waits for them, and re-layouts: 24.7 us -> none  [degree_rows(): lax.scan(block_step, (empty_state, empty_state), jnp.arange(block_count,...]
    pallas_call x0 -> x2, Pallas kernels: none -> 18.5 us  [the longest x1 11.8 us: degree_call(): pl.pallas_call(degree_kernel, out_shape=[jax.ShapeDtypeStruct((SUBLANES,...]
    unnamed x7 -> x4, local copies, waits for them, and re-layouts: 15.6 us -> 2.12 us
    transpose x2 -> x0, local copies, waits for them, and re-layouts: 12.7 us -> none  [the longest x1 11.1 us: degree_rows(): jnp.transpose(parts, (1, 2, 0, 3, 4))]
  transfers between devices with their start and end apart: 1 -> 2, of which waited for: 1 -> 2; matrix products, arithmetic and copies ran while one was open for 1% -> 2% of each run, Pallas kernels for 0% -> 0%
where the time goes in v1:
time: 93.2 us; the launch traced here: 92.9 us
  waiting for transfers between devices  48.8 us (52%)
  Pallas kernels  18.5 us (20%)
  starting transfers between devices  18.3 us (20%)
  local copies, waits for them, and re-layouts  4.16 us (4%)
  other arithmetic  2.32 us (2%)
    all_to_all x1, waiting for transfers between devices, fast_local(): lax.all_to_all(sent, 'beta', split_axis=0, concat_axis=0, tiled=True)  41.5 us
    pallas_call x1, Pallas kernels, degree_call(): pl.pallas_call(degree_kernel, out_shape=[jax.ShapeDtypeStruct((SUBLANES,...  11.8 us
    all_to_all x1, starting transfers between devices, fast_local(): lax.all_to_all(shares, 'beta', split_axis=0, concat_axis=0, tiled=True)  10 us
    all_to_all x1, starting transfers between devices, fast_local(): lax.all_to_all(sent, 'beta', split_axis=0, concat_axis=0, tiled=True)  8.34 us
    all_to_all x1, waiting for transfers between devices, fast_local(): lax.all_to_all(shares, 'beta', split_axis=0, concat_axis=0, tiled=True)  7.32 us
    pallas_call x1, Pallas kernels, spectrum_call(): pl.pallas_call(spectrum_kernel, grid=(functions,), in_specs=[pl.BlockSpec...  6.67 us
    unnamed x4, local copies, waits for them, and re-layouts  2.12 us
  transfers between devices with their start and end apart: 2, of which 2 were waited for; matrix products, arithmetic and copies ran while one was open for 2% of the time, Pallas kernels for 0%

profile of v1, /device:TPU:0, one launch (start us, length us, event | category | flops | bytes accessed | tf_op | source)
XLA Modules:
  0.0 92.9 jit_solution(3483196940068749780)
XLA Ops:
  0.6 6.7 %spectrum.1 = f32[16,4,64,128]{3,2,1,0:T(8,128)} custom-call(f32[8,4,128,128]{3,2,1,0:T(8,128)} %x_ref.1, bf16[128,256]{1,0:T(8,128)(2,1)} %constant.38.clone.gamma_hi, bf16[128,256]{1,0:T(8,128)(2,1)} %constant.39.clone.gamma_lo, bf16[128,256]{1,0:T(8,128)(2,1)} %constant.40.clone.alpha_hi, bf16[128,256]{1,0:T(8,128)(2,1)} %constant.41.clone.alpha_lo), custom_call_target="tpu_custom_call" | custom-call | tf_op jit(solution)/shard_map/spectrum/pallas_call | solution.py:310
  7.3 8.3 %all-to-all-start = ((f32[16,4,64,128]{3,2,1,0:T(8,128)}), f32[16,4,64,128]{3,2,1,0:T(8,128)S(1)}, u32[]{:S(2)}, u32[]{:S(2)}) async-start(f32[16,4,64,128]{3,2,1,0:T(8,128)} %spectrum.1), calls=%async_computation | async-start | bytes 4194304 | tf_op jit(solution)/shard_map/all_to_all | solution.py:408
  15.7 1.5 %dynamic-slice_bitcast_fusion.alpha_ref = f32[20,8,128]{2,1,0:T(8,128)} fusion(f32[16,20,8,128]{3,2,1,0:T(8,128)} %constant.42.clone, s32[]{:T(128)S(6)} %select_n.4), kind=kLoop, calls=%fused_computation | loop fusion | bytes 163844 | tf_op jit(solution)/shard_map/jit(dynamic_index_in_dim)/squeeze | solution.py:410
  17.2 41.5 %all-to-all-done.r_ref = f32[16,4,64,128]{3,2,1,0:T(8,128)S(1)} async-done(((f32[16,4,64,128]{3,2,1,0:T(8,128)}), f32[16,4,64,128]{3,2,1,0:T(8,128)S(1)}, u32[]{:S(2)}, u32[]{:S(2)}) %all-to-all-start) | async-done | bytes 2097184 | tf_op jit(solution)/shard_map/all_to_all | solution.py:408
  58.7 0.0 copy-start
  58.7 1.3 %copy-done = f32[16,4,64,128]{3,2,1,0:T(8,128)} copy-done((f32[16,4,64,128]{3,2,1,0:T(8,128)}, f32[16,4,64,128]{3,2,1,0:T(8,128)S(1)}, u32[]{:S(2)}) %copy-start) | copy-done | bytes 2097176
  60.0 11.8 %degrees.1 = (f32[8,2,4,64,64]{4,3,2,1,0:T(8,128)}, f32[4,64,128]{2,1,0:T(8,128)}) custom-call(f32[16,4,64,128]{3,2,1,0:T(8,128)} %copy-done, bf16[64,256]{1,0:T(8,128)(2,1)} %constant.44.clone.beta_hi, bf16[64,256]{1,0:T(8,128)(2,1)} %constant.45.clone.beta_lo, bf16[8,128]{1,0:T(8,128)(2,1)} %constant.46.clone.even_ref, ...), custom_call_target="tpu_custom_call" | custom-call | tf_op jit(solution)/shard_map/degrees/pallas_call | solution.py:388
  71.9 1.0 %reduce_sum.18 = f32[4,64]{1,0:T(4,128)S(1)} reduce(f32[4,64,128]{2,1,0:T(8,128)} %get-tuple-element.5, f32[]{:T(128)} %constant.35.clone.1), dimensions={2}, to_apply=%region_0.1 | reduce | flops 32512 | bytes 132100 | tf_op jit(solution)/shard_map/reduce_sum | solution.py:412
  72.9 0.7 reshape.11
  73.6 10.0 %all-to-all-start.1 = ((f32[16,1,256]{2,1,0:T(1,128)}), f32[16,1,256]{2,1,0:T(1,128)S(1)}, u32[]{:S(2)}, u32[]{:S(2)}) async-start(f32[16,1,256]{2,1,0:T(1,128)} %reshape.11), calls=%async_computation.1 | async-start | bytes 32768 | tf_op jit(solution)/shard_map/all_to_all | solution.py:414
  83.6 7.3 %all-to-all-done.1 = f32[16,1,256]{2,1,0:T(1,128)S(1)} async-done(((f32[16,1,256]{2,1,0:T(1,128)}), f32[16,1,256]{2,1,0:T(1,128)S(1)}, u32[]{:S(2)}, u32[]{:S(2)}) %all-to-all-start.1) | async-done | bytes 16416 | tf_op jit(solution)/shard_map/all_to_all | solution.py:414
  91.0 0.5 broadcast.9
  91.5 0.7 reduce
  92.2 0.1 reshape.12
  92.3 0.6 broadcast_divide_fusion
  (3 shorter events, 0.0 us)
Async XLA Ops:
  7.3 51.4 %all-to-all-start = ((f32[16,4,64,128]{3,2,1,0:T(8,128)}), f32[16,4,64,128]{3,2,1,0:T(8,128)S(1)}, u32[]{:S(2)}, u32[]{:S(2)}) async-start(f32[16,4,64,128]{3,2,1,0:T(8,128)} %spectrum.1), calls=%async_computation | async-start | bytes 4194304 | tf_op jit(solution)/shard_map/all_to_all | solution.py:408
  58.7 1.4 %copy-start = (f32[16,4,64,128]{3,2,1,0:T(8,128)}, f32[16,4,64,128]{3,2,1,0:T(8,128)S(1)}, u32[]{:S(2)}) copy-start(f32[16,4,64,128]{3,2,1,0:T(8,128)S(1)} %all-to-all-done.r_ref) | copy-start | bytes 6291460
  73.6 17.3 %all-to-all-start.1 = ((f32[16,1,256]{2,1,0:T(1,128)}), f32[16,1,256]{2,1,0:T(1,128)S(1)}, u32[]{:S(2)}, u32[]{:S(2)}) async-start(f32[16,1,256]{2,1,0:T(1,128)} %reshape.11), calls=%async_computation.1 | async-start | bytes 32768 | tf_op jit(solution)/shard_map/all_to_all | solution.py:414

commit v2 on v1

--- a/solution.py
+++ b/solution.py
@@ -250,31 +250,28 @@
 
 
 def block_steps(spread):
-    width = LANES // SUBLANES
-    return [
-        (block, chunk)
-        for block in range(spread // SUBLANES)
-        for chunk in range(-(-(block + 1) * SUBLANES // width))
-    ]
+    blocks = spread // SUBLANES
+    return [(block, chunk) for block in range(blocks) for chunk in range(block + 1)]
 
 
 def quarter_tables(spread, devices):
     quarter = wigner_quarter(spread)
-    grid, width = 2 * spread, LANES // SUBLANES
-    rows = np.arange(grid)
-    orders = np.where(rows < spread, rows, rows - grid)
-    held = np.clip(orders + spread - 1, 0, 2 * spread - 2)
-    by_row = np.where((orders > -spread)[None, :, None], quarter[:, held, :], 0.0)
+    rows = np.arange(2 * spread)
+    orders = np.where(rows < spread, rows, rows - 2 * spread)
+    by_row = quarter[:, np.maximum(orders, 1 - spread) + spread - 1, :]
+    by_row = np.where((orders > -spread)[None, :, None], by_row, 0.0)
     by_row = by_row * (8.0 * np.sqrt(2.0 * np.arange(spread) + 1.0))[:, None, None]
     gammas, alphas = [], []
     for block, chunk in block_steps(spread):
         degrees = slice(block * SUBLANES, (block + 1) * SUBLANES)
-        part = slice(chunk * width, (chunk + 1) * width)
-        table = np.swapaxes(quarter[degrees, spread - 1 :, part], 1, 2).reshape(LANES, spread)
+        part = slice(chunk * SUBLANES, (chunk + 1) * SUBLANES)
+        table = np.swapaxes(quarter[degrees, spread - 1 :, part], 1, 2).reshape(-1, spread)
         gammas.append(np.concatenate([table, table], axis=1))
-        table = np.swapaxes(by_row[degrees, :, part], 0, 1).reshape(devices, SUBLANES, LANES)
-        alphas.append(table)
-    return np.stack(gammas).astype(np.float32), np.stack(alphas, axis=1).astype(np.float32)
+        table = np.swapaxes(by_row[degrees, :, part], 0, 1)
+        alphas.append(table.reshape(devices, SUBLANES, SUBLANES * SUBLANES))
+    alphas = np.stack(alphas, axis=1)
+    alphas = np.concatenate([alphas[:, 0::2], alphas[:, 1::2]], axis=-1)
+    return np.stack(gammas).astype(np.float32), alphas.astype(np.float32)
 
 
 def split_value(value):
@@ -286,25 +283,34 @@
     return jnp.dot(left, right, preferred_element_type=jnp.float32)
 
 
-def spectrum_kernel(x_ref, gamma_hi, gamma_lo, alpha_hi, alpha_lo, out_ref):
+def spectrum_kernel(x_ref, gamma_two, gamma_lo, alpha_hi, alpha_lo, out_ref):
     count, _, grid, _ = x_ref.shape
     blocks = out_ref.shape[0]
-    for k in range(count):
-        high, low = split_value(x_ref[k, 0])
-        half = dot(high, gamma_hi[...]) + dot(low, gamma_hi[...]) + dot(high, gamma_lo[...])
-        pair = jnp.concatenate([half[:, :LANES], half[:, LANES:]], axis=0)
+    high, low = split_value(x_ref[:, 0].reshape(count * grid, grid))
+    half = dot(jnp.concatenate([high, low], axis=1), gamma_two[...]) + dot(high, gamma_lo[...])
+    for k in range(0, count, 2):
+        pairs = [half[(k + i) * grid : (k + i + 1) * grid] for i in range(2)]
+        pair = jnp.concatenate(
+            [
+                jnp.concatenate([p[:, :LANES] for p in pairs], axis=1),
+                jnp.concatenate([p[:, LANES:] for p in pairs], axis=1),
+            ],
+            axis=0,
+        )
         high, low = split_value(pair)
         rows = dot(alpha_hi[...], high) + dot(alpha_lo[...], high) + dot(alpha_hi[...], low)
-        for d in range(blocks):
-            out_ref[d, 0, pl.ds(k, SUBLANES, stride=count), :] = rows[
-                d * SUBLANES : (d + 1) * SUBLANES
-            ]
+        for i in range(2):
+            for d in range(blocks):
+                out_ref[d, 0, pl.ds(k + i, SUBLANES, stride=count), :] = rows[
+                    d * SUBLANES : (d + 1) * SUBLANES, i * LANES : (i + 1) * LANES
+                ]
 
 
 def spectrum_call(samples, devices):
     count, functions, grid, _ = samples.shape
     gamma_part, alpha_part = fourier_tables(grid // 2)
-    tables = [*split_pair(gamma_part), *split_pair(alpha_part)]
+    gamma_hi, gamma_lo = split_pair(gamma_part)
+    tables = [np.concatenate([gamma_hi, gamma_hi], axis=0), gamma_lo, *split_pair(alpha_part)]
     rows = grid // devices * count
     whole = lambda table: pl.BlockSpec(table.shape, lambda f: (0, 0))
     return pl.pallas_call(
@@ -318,13 +324,49 @@
     )(samples, *tables)
 
 
+def factor_kernel(gamma_ref, alpha_ref, out_ref):
+    pairs = out_ref.shape[1]
+
+    def step(at, carry):
+        column = alpha_ref[at]
+        for half in range(2):
+            for i in range(pairs):
+                lane = half * pairs + i
+                row = gamma_ref[2 * at + half, pl.ds(i, SUBLANES, stride=0), :]
+                wide = jnp.broadcast_to(column[:, lane : lane + 1], (SUBLANES, LANES))
+                out_ref[2 * at + half, i] = wide * row
+        return carry
+
+    lax.fori_loop(0, alpha_ref.shape[0], step, 0)
+
+
+def factor_call(gammas, alphas):
+    steps, pairs, _ = gammas.shape
+    return pl.pallas_call(
+        factor_kernel,
+        out_shape=jax.ShapeDtypeStruct((steps, pairs, SUBLANES, LANES), jnp.float32),
+        name="factors",
+    )(gammas, alphas)
+
+
 def degree_kernel(
-    r_ref, beta_hi, beta_lo, even_ref, odd_ref, gamma_ref, alpha_ref, out_ref, pow_ref, t_ref, c_ref
+    r_ref, beta_hi, beta_lo, even_ref, odd_ref, source_ref, out_ref, pow_ref,
+    t_ref, c_ref, e_ref, held_ref, factor_ref, sems, factor_sems,
 ):
     sources, functions, held, _ = r_ref.shape
     count = held // SUBLANES
     spread = beta_hi.shape[0]
-    width = LANES // SUBLANES
+    blocks = spread // SUBLANES
+    firsts = [block * (block + 1) // 2 for block in range(blocks)]
+
+    def factor_copy(block):
+        part = pl.ds(firsts[block], block + 1)
+        return pltpu.make_async_copy(
+            source_ref.at[part], factor_ref.at[part], factor_sems.at[block]
+        )
+
+    for block in range(blocks):
+        factor_copy(block).start()
     for f in range(0, functions, 2):
         for n in range(SUBLANES):
             parts = [
@@ -338,34 +380,33 @@
             low = jnp.concatenate([low * even, low * odd], axis=0)
             turned = dot(beta_hi[...], high) + dot(beta_lo[...], high) + dot(beta_hi[...], low)
             for i in range(2):
-                for b in range(spread // SUBLANES):
+                for b in range(blocks):
                     t_ref[f + i, pl.ds(b * SUBLANES * SUBLANES + n, SUBLANES, stride=SUBLANES), :] = (
                         turned[b * SUBLANES : (b + 1) * SUBLANES, i * LANES : (i + 1) * LANES]
                     )
 
-    lane = lax.broadcasted_iota(jnp.int32, (SUBLANES, LANES), 1)
-    fold = jnp.where(lane % spread == 0, 1.0, 2.0).astype(jnp.float32)
-
-    def block_step(block, first):
-        chunks = (block * SUBLANES + SUBLANES + width - 1) // width
+    zero = jnp.zeros((SUBLANES, LANES), jnp.float32)
+
+    def out_copy(block):
+        part = (slice(None), slice(None), slice(None), pl.ds(block * SUBLANES, SUBLANES))
+        return pltpu.make_async_copy(held_ref.at[part], out_ref.at[part], sems.at[block])
+
+    for block in range(blocks):
+        factor_copy(block).wait()
 
         def chunk_step(chunk, totals):
             totals = list(totals)
-            column = alpha_ref[first + chunk]
-            for m in range(width):
-                row = pl.multiple_of((chunk * width + m) * SUBLANES, SUBLANES)
+            for m in range(SUBLANES):
+                row = pl.multiple_of((chunk * SUBLANES + m) * SUBLANES, SUBLANES)
                 values = [t_ref[f, pl.ds(row, SUBLANES), :] for f in range(functions)]
                 for j in range(SUBLANES):
-                    at = j * width + m
-                    table = gamma_ref[first + chunk, pl.ds(at, SUBLANES, stride=0), :]
-                    factor = jnp.broadcast_to(column[:, at : at + 1], (SUBLANES, LANES)) * table
+                    factor = factor_ref[firsts[block] + chunk, j * SUBLANES + m]
                     for f in range(functions):
                         totals[j * functions + f] += factor * values[f]
             return tuple(totals)
 
-        zero = jnp.zeros((SUBLANES, LANES), jnp.float32)
-        totals = lax.fori_loop(0, chunks, chunk_step, (zero,) * (SUBLANES * functions))
-        degree = pl.multiple_of(block * SUBLANES, SUBLANES)
+        totals = lax.fori_loop(0, block + 1, chunk_step, (zero,) * (SUBLANES * functions))
+        degrees = slice(block * SUBLANES, (block + 1) * SUBLANES)
         for f in range(functions):
             for j in range(SUBLANES):
                 c_ref[f, pl.ds(j, SUBLANES, stride=SUBLANES), :] = totals[j * functions + f]
@@ -373,30 +414,56 @@
             for n in range(SUBLANES):
                 tile = c_ref[f, n * SUBLANES : (n + 1) * SUBLANES, :]
                 energy += tile * tile
-                out_ref[n, 0, f, pl.ds(degree, SUBLANES), :] = tile[:, :spread]
-                out_ref[n, 1, f, pl.ds(degree, SUBLANES), :] = tile[:, spread:]
-            pow_ref[f, pl.ds(degree, SUBLANES), :] = energy * fold
-        return first + chunks
-
-    lax.fori_loop(0, spread // SUBLANES, block_step, 0)
-
-
-def degree_call(received, gammas, alphas, spread):
+                held_ref[n, 0, f, degrees, :] = tile[:, :spread]
+                held_ref[n, 1, f, degrees, :] = tile[:, spread:]
+            e_ref[f, degrees, :] = energy
+        out_copy(block).start()
+
+    lane = lax.broadcasted_iota(jnp.int32, (SUBLANES, LANES), 1)
+    fold = jnp.where(lane % spread == 0, 1.0, 2.0).astype(jnp.bfloat16)
+    across = lambda part: lax.dot_general(
+        fold, part, (((1,), (1,)), ((), ())), preferred_element_type=jnp.float32
+    )
+    place = lax.broadcasted_iota(jnp.int32, (SUBLANES, spread), 0)
+    power = jnp.zeros((SUBLANES, spread), jnp.float32)
+    for f in range(functions):
+        high, low = split_value(e_ref[f])
+        rest = e_ref[f] - high.astype(jnp.float32) - low.astype(jnp.float32)
+        total = across(high) + across(low) + across(rest.astype(jnp.bfloat16))
+        power = jnp.where(place == f, total, power)
+    pow_ref[:, :spread] = power
+    pow_ref[:, spread:] = jnp.zeros_like(power)
+
+    for block in range(blocks):
+        out_copy(block).wait()
+
+
+def degree_call(received, factors, spread):
     functions = received.shape[1]
     tables = [*split_pair(beta_table(spread))]
     tables += [mask.astype(jnp.bfloat16) for mask in sign_masks(spread)]
+    shape = (SUBLANES, 2, functions, spread, spread)
+    vmem = pl.BlockSpec(memory_space=pltpu.VMEM)
     return pl.pallas_call(
         degree_kernel,
+        in_specs=[vmem] * 5 + [pl.BlockSpec(memory_space=pl.ANY)],
+        out_specs=[pl.BlockSpec(memory_space=pl.ANY), vmem],
         out_shape=[
-            jax.ShapeDtypeStruct((SUBLANES, 2, functions, spread, spread), jnp.float32),
-            jax.ShapeDtypeStruct((functions, spread, LANES), jnp.float32),
+            jax.ShapeDtypeStruct(shape, jnp.float32),
+            jax.ShapeDtypeStruct((SUBLANES, LANES), jnp.float32),
         ],
         scratch_shapes=[
             pltpu.VMEM((functions, spread * SUBLANES, LANES), jnp.float32),
             pltpu.VMEM((functions, SUBLANES * SUBLANES, LANES), jnp.float32),
+            pltpu.VMEM((functions, spread, LANES), jnp.float32),
+            pltpu.VMEM(shape, jnp.float32),
+            pltpu.VMEM(factors.shape, jnp.float32),
+            pltpu.SemaphoreType.DMA((spread // SUBLANES,)),
+            pltpu.SemaphoreType.DMA((spread // SUBLANES,)),
         ],
+        compiler_params=pltpu.CompilerParams(vmem_limit_bytes=50 << 20),
         name="degrees",
-    )(received, *tables, gammas, alphas)
+    )(received, *tables, factors)
 
 
 def fast_local(samples):
@@ -408,12 +475,13 @@
     received = lax.all_to_all(sent, "beta", split_axis=0, concat_axis=0, tiled=True)
     gammas, alphas = quarter_tables(spread, devices)
     alphas = lax.dynamic_index_in_dim(jnp.asarray(alphas), device, 0, keepdims=False)
-    coeffs, energy = degree_call(received, jnp.asarray(gammas), alphas, spread)
-    share = jnp.sum(energy, axis=-1)
-    shares = jnp.broadcast_to(share[None], (devices, functions, spread))
+    factors = factor_call(jnp.asarray(gammas), alphas)
+    coeffs, share = degree_call(received, factors, spread)
+    shares = jnp.broadcast_to(share[None], (devices,) + share.shape)
     shares = lax.all_to_all(shares, "beta", split_axis=0, concat_axis=0, tiled=True)
     degrees = 2.0 * jnp.arange(spread, dtype=jnp.float32) + 1.0
-    return coeffs, jnp.sum(shares, axis=0) / (degrees * degrees)[None, :]
+    energy = jnp.sum(shares[:, :functions, :spread], axis=0)
+    return coeffs, energy / (degrees * degrees)[None, :]
 
 
 def local(samples):

time: 93.2 us -> 84.3 us (0.905)
  waiting for transfers between devices: 48.8 us -> 38.8 us
  Pallas kernels: 18.5 us -> 23.2 us
  local copies, waits for them, and re-layouts: 4.16 us -> 2.17 us
  other arithmetic: 2.32 us -> 0.62 us
    all_to_all x1, waiting for transfers between devices: 41.5 us -> 31.3 us  [fast_local(): lax.all_to_all(sent, 'beta', split_axis=0, concat_axis=0, tiled=True)]
    pallas_call x1 -> x2, Pallas kernels: 11.8 us -> 17.2 us  [the longest x1 10.2 us: factor_call(): pl.pallas_call(factor_kernel, out_shape=jax.ShapeDtypeStruct((steps, pair...]
    unnamed x4 -> x8, local copies, waits for them, and re-layouts: 2.12 us -> 0.01 us
    reduce_sum x2 -> x1, other arithmetic: 1.04 us -> 0.03 us  [fast_local(): energy = jnp.sum(shares[:, :functions, :spread], axis=0)]
  transfers between devices with their start and end apart: 2 -> 2, of which waited for: 2 -> 2; matrix products, arithmetic and copies ran while one was open for 2% -> 2% of each run, Pallas kernels for 0% -> 12%
where the time goes in v2:
time: 84.3 us; the launch traced here: 83.9 us
  waiting for transfers between devices  38.8 us (46%)
  Pallas kernels  23.2 us (28%)
  starting transfers between devices  18.3 us (22%)
  local copies, waits for them, and re-layouts  2.17 us (3%)
    all_to_all x1, waiting for transfers between devices, fast_local(): lax.all_to_all(sent, 'beta', split_axis=0, concat_axis=0, tiled=True)  31.3 us
    pallas_call x1, Pallas kernels, factor_call(): pl.pallas_call(factor_kernel, out_shape=jax.ShapeDtypeStruct((steps, pair...  10.2 us
    all_to_all x1, starting transfers between devices, fast_local(): lax.all_to_all(shares, 'beta', split_axis=0, concat_axis=0, tiled=True)  10 us
    all_to_all x1, starting transfers between devices, fast_local(): lax.all_to_all(sent, 'beta', split_axis=0, concat_axis=0, tiled=True)  8.34 us
    all_to_all x1, waiting for transfers between devices, fast_local(): lax.all_to_all(shares, 'beta', split_axis=0, concat_axis=0, tiled=True)  7.52 us
    pallas_call x1, Pallas kernels, degree_call(): pl.pallas_call(degree_kernel, in_specs=[vmem] * 5 + [pl.BlockSpec(memory_...  6.98 us
    pallas_call x1, Pallas kernels, spectrum_call(): pl.pallas_call(spectrum_kernel, grid=(functions,), in_specs=[pl.BlockSpec...  6.07 us
  transfers between devices with their start and end apart: 2, of which 2 were waited for; matrix products, arithmetic and copies ran while one was open for 2% of the time, Pallas kernels for 12%

profile of v2, /device:TPU:0, one launch (start us, length us, event | category | flops | bytes accessed | tf_op | source)
XLA Modules:
  0.0 83.9 jit_solution(9148322720672173805)
XLA Ops:
  0.6 6.1 %spectrum.1 = f32[16,4,64,128]{3,2,1,0:T(8,128)} custom-call(f32[8,4,128,128]{3,2,1,0:T(8,128)} %x_ref.1, bf16[256,256]{1,0:T(8,128)(2,1)} %constant.38.clone.gamma_two, bf16[128,256]{1,0:T(8,128)(2,1)} %constant.39.clone.gamma_lo, bf16[128,256]{1,0:T(8,128)(2,1)} %constant.40.clone.alpha_hi, bf16[128,256]{1,0:T(8,128)(2,1)} %constant.41.clone.alpha_lo), custom_call_target="tpu_custom_call" | custom-call | tf_op jit(solution)/shard_map/spectrum/pallas_call | solution.py:316
  6.7 8.3 %all-to-all-start = ((f32[16,4,64,128]{3,2,1,0:T(8,128)}), f32[16,4,64,128]{3,2,1,0:T(8,128)S(1)}, u32[]{:S(2)}, u32[]{:S(2)}) async-start(f32[16,4,64,128]{3,2,1,0:T(8,128)} %spectrum.1), calls=%async_computation | async-start | bytes 4194304 | tf_op jit(solution)/shard_map/all_to_all | solution.py:475
  15.1 1.5 %dynamic-slice_bitcast_fusion.alpha_ref = f32[18,8,128]{2,1,0:T(8,128)} fusion(f32[16,18,8,128]{3,2,1,0:T(8,128)} %constant.42.clone, s32[]{:T(128)S(6)} %select_n.4), kind=kLoop, calls=%fused_computation | loop fusion | bytes 147460 | tf_op jit(solution)/shard_map/jit(dynamic_index_in_dim)/squeeze | solution.py:477
  16.6 0.0 copy-start
  16.6 0.0 copy-start.1
  16.6 0.0 copy-start.2
  16.6 0.0 copy-start.3
  16.6 10.2 %factors.1.source_ref = f32[36,64,8,128]{3,2,1,0:T(8,128)} custom-call(f32[36,64,128]{2,1,0:T(8,128)} %constant.43.clone.gamma_ref, f32[18,8,128]{2,1,0:T(8,128)} %dynamic-slice_bitcast_fusion.alpha_ref), custom_call_target="tpu_custom_call" | custom-call | tf_op jit(solution)/shard_map/factors/pallas_call | solution.py:345
  26.8 31.3 %all-to-all-done.r_ref = f32[16,4,64,128]{3,2,1,0:T(8,128)S(1)} async-done(((f32[16,4,64,128]{3,2,1,0:T(8,128)}), f32[16,4,64,128]{3,2,1,0:T(8,128)S(1)}, u32[]{:S(2)}, u32[]{:S(2)}) %all-to-all-start) | async-done | bytes 2097184 | tf_op jit(solution)/shard_map/all_to_all | solution.py:475
  58.1 0.0 copy-done
  58.1 0.0 copy-done.1
  58.1 0.0 copy-done.2
  58.1 0.0 copy-done.3
  58.1 7.0 %degrees.1 = (f32[8,2,4,64,64]{4,3,2,1,0:T(8,128)}, f32[8,128]{1,0:T(8,128)S(1)}) custom-call(f32[16,4,64,128]{3,2,1,0:T(8,128)S(1)} %all-to-all-done.r_ref, bf16[64,256]{1,0:T(8,128)(2,1)S(1)} %copy-done, bf16[64,256]{1,0:T(8,128)(2,1)S(1)} %copy-done.1, bf16[8,128]{1,0:T(8,128)(2,1)S(1)} %copy-done.2, bf16[8,128]{1,0:T(8,128)(2,1)S(1)} %copy-done.3, ...), custom_call_target="tpu_custom_call" | custom-call | tf_op jit(solution)/shard_map/degrees/pallas_call | solution.py:447
  65.1 0.6 broadcast_in_dim.2
  65.7 10.0 %all-to-all-start.1 = ((f32[16,8,128]{2,1,0:T(8,128)}), f32[16,8,128]{2,1,0:T(8,128)S(1)}, u32[]{:S(2)}, u32[]{:S(2)}) async-start(f32[16,8,128]{2,1,0:T(8,128)} %broadcast_in_dim.2), calls=%async_computation.1 | async-start | bytes 131072 | tf_op jit(solution)/shard_map/all_to_all | solution.py:481
  75.8 7.5 %all-to-all-done.1 = f32[16,8,128]{2,1,0:T(8,128)S(1)} async-done(((f32[16,8,128]{2,1,0:T(8,128)}), f32[16,8,128]{2,1,0:T(8,128)S(1)}, u32[]{:S(2)}, u32[]{:S(2)}) %all-to-all-start.1) | async-done | bytes 65568 | tf_op jit(solution)/shard_map/all_to_all | solution.py:481
  83.3 0.6 broadcast_divide_fusion
  (2 shorter events, 0.0 us)
Async XLA Ops:
  6.7 51.4 %all-to-all-start = ((f32[16,4,64,128]{3,2,1,0:T(8,128)}), f32[16,4,64,128]{3,2,1,0:T(8,128)S(1)}, u32[]{:S(2)}, u32[]{:S(2)}) async-start(f32[16,4,64,128]{3,2,1,0:T(8,128)} %spectrum.1), calls=%async_computation | async-start | bytes 4194304 | tf_op jit(solution)/shard_map/all_to_all | solution.py:475
  16.6 41.5 %copy-start = (bf16[64,256]{1,0:T(8,128)(2,1)S(1)}, bf16[64,256]{1,0:T(8,128)(2,1)}, u32[]{:S(2)}) copy-start(bf16[64,256]{1,0:T(8,128)(2,1)} %constant.44.clone.beta_hi) | copy-start | bytes 98308
  16.6 41.5 %copy-start.1 = (bf16[64,256]{1,0:T(8,128)(2,1)S(1)}, bf16[64,256]{1,0:T(8,128)(2,1)}, u32[]{:S(2)}) copy-start(bf16[64,256]{1,0:T(8,128)(2,1)} %constant.45.clone.beta_lo) | copy-start | bytes 98308
  16.6 41.5 %copy-start.2 = (bf16[8,128]{1,0:T(8,128)(2,1)S(1)}, bf16[8,128]{1,0:T(8,128)(2,1)}, u32[]{:S(2)}) copy-start(bf16[8,128]{1,0:T(8,128)(2,1)} %constant.46.clone.even_ref) | copy-start | bytes 6148
  16.6 41.5 %copy-start.3 = (bf16[8,128]{1,0:T(8,128)(2,1)S(1)}, bf16[8,128]{1,0:T(8,128)(2,1)}, u32[]{:S(2)}) copy-start(bf16[8,128]{1,0:T(8,128)(2,1)} %constant.47.clone.odd_ref) | copy-start | bytes 6148
  65.7 17.5 %all-to-all-start.1 = ((f32[16,8,128]{2,1,0:T(8,128)}), f32[16,8,128]{2,1,0:T(8,128)S(1)}, u32[]{:S(2)}, u32[]{:S(2)}) async-start(f32[16,8,128]{2,1,0:T(8,128)} %broadcast_in_dim.2), calls=%async_computation.1 | async-start | bytes 131072 | tf_op jit(solution)/shard_map/all_to_all | solution.py:481

commit v3 on v2

--- a/solution.py
+++ b/solution.py
@@ -236,10 +236,10 @@
     odd = 2.0 * np.arange(spread) + 1.0
     series = np.sum(np.sin(angles[:, None] * odd[None, :]) / odd[None, :], axis=1)
     weight = 2.0 / spread * np.sin(angles) * series
-    order = np.arange(spread)
+    order = np.concatenate([np.arange(0, spread, 2), np.arange(1, spread, 2)])
     fold = np.where(order == 0, 1.0, 2.0)[:, None] * weight[None, :]
     turn = order[:, None] * angles[None, :]
-    return np.concatenate([fold * np.cos(turn), fold * np.sin(turn)], axis=1)
+    return np.concatenate([fold * np.cos(turn), fold * np.sin(turn)], axis=0)
 
 
 def sign_masks(spread):
@@ -265,8 +265,7 @@
     for block, chunk in block_steps(spread):
         degrees = slice(block * SUBLANES, (block + 1) * SUBLANES)
         part = slice(chunk * SUBLANES, (chunk + 1) * SUBLANES)
-        table = np.swapaxes(quarter[degrees, spread - 1 :, part], 1, 2).reshape(-1, spread)
-        gammas.append(np.concatenate([table, table], axis=1))
+        gammas.append(np.swapaxes(quarter[degrees, spread - 1 :, part], 1, 2).reshape(-1, LANES))
         table = np.swapaxes(by_row[degrees, :, part], 0, 1)
         alphas.append(table.reshape(devices, SUBLANES, SUBLANES * SUBLANES))
     alphas = np.stack(alphas, axis=1)
@@ -283,7 +282,7 @@
     return jnp.dot(left, right, preferred_element_type=jnp.float32)
 
 
-def spectrum_kernel(x_ref, gamma_two, gamma_lo, alpha_hi, alpha_lo, out_ref):
+def spectrum_kernel(x_ref, gamma_two, gamma_lo, alpha_two, out_ref):
     count, _, grid, _ = x_ref.shape
     blocks = out_ref.shape[0]
     high, low = split_value(x_ref[:, 0].reshape(count * grid, grid))
@@ -298,7 +297,8 @@
             axis=0,
         )
         high, low = split_value(pair)
-        rows = dot(alpha_hi[...], high) + dot(alpha_lo[...], high) + dot(alpha_hi[...], low)
+        both = dot(alpha_two[...], high)
+        rows = both[:grid] + both[grid:] + dot(alpha_two[:grid], low)
         for i in range(2):
             for d in range(blocks):
                 out_ref[d, 0, pl.ds(k + i, SUBLANES, stride=count), :] = rows[
@@ -310,7 +310,8 @@
     count, functions, grid, _ = samples.shape
     gamma_part, alpha_part = fourier_tables(grid // 2)
     gamma_hi, gamma_lo = split_pair(gamma_part)
-    tables = [np.concatenate([gamma_hi, gamma_hi], axis=0), gamma_lo, *split_pair(alpha_part)]
+    tables = [np.concatenate([gamma_hi, gamma_hi], axis=0), gamma_lo]
+    tables.append(np.concatenate(split_pair(alpha_part), axis=0))
     rows = grid // devices * count
     whole = lambda table: pl.BlockSpec(table.shape, lambda f: (0, 0))
     return pl.pallas_call(
@@ -326,15 +327,19 @@
 
 def factor_kernel(gamma_ref, alpha_ref, out_ref):
     pairs = out_ref.shape[1]
+    left = lax.broadcasted_iota(jnp.int32, (SUBLANES, LANES), 1) < LANES // 2
 
     def step(at, carry):
         column = alpha_ref[at]
         for half in range(2):
             for i in range(pairs):
-                lane = half * pairs + i
+                lane = 2 * (half * pairs + i)
+                wide = [
+                    jnp.broadcast_to(column[:, lane + j : lane + j + 1], (SUBLANES, LANES))
+                    for j in range(2)
+                ]
                 row = gamma_ref[2 * at + half, pl.ds(i, SUBLANES, stride=0), :]
-                wide = jnp.broadcast_to(column[:, lane : lane + 1], (SUBLANES, LANES))
-                out_ref[2 * at + half, i] = wide * row
+                out_ref[2 * at + half, i] = jnp.where(left, wide[0], wide[1]) * row
         return carry
 
     lax.fori_loop(0, alpha_ref.shape[0], step, 0)
@@ -350,12 +355,12 @@
 
 
 def degree_kernel(
-    r_ref, beta_hi, beta_lo, even_ref, odd_ref, source_ref, out_ref, pow_ref,
+    r_ref, beta_two, even_ref, odd_ref, source_ref, out_ref, pow_ref,
     t_ref, c_ref, e_ref, held_ref, factor_ref, sems, factor_sems,
 ):
     sources, functions, held, _ = r_ref.shape
     count = held // SUBLANES
-    spread = beta_hi.shape[0]
+    spread = beta_two.shape[0] // 4
     blocks = spread // SUBLANES
     firsts = [block * (block + 1) // 2 for block in range(blocks)]
 
@@ -365,8 +370,16 @@
             source_ref.at[part], factor_ref.at[part], factor_sems.at[block]
         )
 
+    row = lax.axis_index("beta") * SUBLANES
+    smallest = jnp.where(row < spread, row, 2 * spread - row - SUBLANES + 1)
+    first_block = smallest // SUBLANES
     for block in range(blocks):
-        factor_copy(block).start()
+
+        @pl.when(block >= first_block)
+        def _():
+            factor_copy(block).start()
+
+    left = lax.broadcasted_iota(jnp.int32, (spread // 2, LANES), 1) < spread
     for f in range(0, functions, 2):
         for n in range(SUBLANES):
             parts = [
@@ -374,16 +387,27 @@
                 for i in range(2)
             ]
             high, low = split_value(jnp.concatenate(parts, axis=1))
-            even = jnp.concatenate([even_ref[n : n + 1, :]] * 2, axis=1)
-            odd = jnp.concatenate([odd_ref[n : n + 1, :]] * 2, axis=1)
-            high = jnp.concatenate([high * even, high * odd], axis=0)
-            low = jnp.concatenate([low * even, low * odd], axis=0)
-            turned = dot(beta_hi[...], high) + dot(beta_lo[...], high) + dot(beta_hi[...], low)
+            both = dot(beta_two[...], jnp.concatenate([high, low], axis=0))
+            both = both[: 2 * spread] + both[2 * spread :]
+            turned = [
+                jnp.where(
+                    even_ref[n : n + 1] != 0.0,
+                    both[:spread, i * LANES : (i + 1) * LANES] * even_ref[n : n + 1],
+                    both[spread:, i * LANES : (i + 1) * LANES] * odd_ref[n : n + 1],
+                )
+                for i in range(2)
+            ]
             for i in range(2):
-                for b in range(blocks):
-                    t_ref[f + i, pl.ds(b * SUBLANES * SUBLANES + n, SUBLANES, stride=SUBLANES), :] = (
-                        turned[b * SUBLANES : (b + 1) * SUBLANES, i * LANES : (i + 1) * LANES]
-                    )
+                evens, odds = turned[i][: spread // 2], turned[i][spread // 2 :]
+                parted = (
+                    jnp.where(left, evens, pltpu.roll(odds, spread, 1)),
+                    jnp.where(left, pltpu.roll(evens, spread, 1), odds),
+                )
+                for part in range(2):
+                    for b in range(spread // (2 * SUBLANES)):
+                        t_ref[
+                            part, f + i, pl.ds(b * SUBLANES * SUBLANES + n, SUBLANES, stride=SUBLANES), :
+                        ] = parted[part][b * SUBLANES : (b + 1) * SUBLANES]
 
     zero = jnp.zeros((SUBLANES, LANES), jnp.float32)
 
@@ -391,36 +415,49 @@
         part = (slice(None), slice(None), slice(None), pl.ds(block * SUBLANES, SUBLANES))
         return pltpu.make_async_copy(held_ref.at[part], out_ref.at[part], sems.at[block])
 
+    def fill(block):
+        degrees = slice(block * SUBLANES, (block + 1) * SUBLANES)
+        empty = jnp.zeros((SUBLANES, 2, functions, SUBLANES, spread), jnp.float32)
+        held_ref[:, :, :, degrees, :] = empty
+        for f in range(functions):
+            e_ref[f, degrees, :] = zero
+
+    channels = [(part, f) for part in range(2) for f in range(functions)]
+    some = SUBLANES // 2
+
+    def work(block):
+        factor_copy(block).wait()
+        degrees = slice(block * SUBLANES, (block + 1) * SUBLANES)
+        for half in range(2):
+            totals = [[zero] * len(channels) for _ in range(some)]
+            for chunk in range(block + 1):
+                for i in range(SUBLANES // 2):
+                    row = (chunk * SUBLANES // 2 + i) * SUBLANES
+                    values = [t_ref[part, f, row : row + SUBLANES, :] for part, f in channels]
+                    for j in range(some):
+                        at = (half * some + j) * SUBLANES // 2 + i
+                        factor = factor_ref[firsts[block] + chunk, at]
+                        totals[j] = [t + factor * v for t, v in zip(totals[j], values)]
+            for j in range(some):
+                for (part, f), total in zip(channels, totals[j]):
+                    c_ref[part, f, pl.ds(half * some + j, SUBLANES, stride=SUBLANES), :] = total
+        for f in range(functions):
+            energy = zero
+            for part in range(2):
+                for n in range(SUBLANES):
+                    tile = c_ref[part, f, n * SUBLANES : (n + 1) * SUBLANES, :]
+                    tile = tile + pltpu.roll(tile, spread, 1)
+                    energy += tile * tile
+                    held_ref[n, part, f, degrees, :] = tile[:, :spread]
+            e_ref[f, degrees, :] = energy
+
     for block in range(blocks):
-        factor_copy(block).wait()
-
-        def chunk_step(chunk, totals):
-            totals = list(totals)
-            for m in range(SUBLANES):
-                row = pl.multiple_of((chunk * SUBLANES + m) * SUBLANES, SUBLANES)
-                values = [t_ref[f, pl.ds(row, SUBLANES), :] for f in range(functions)]
-                for j in range(SUBLANES):
-                    factor = factor_ref[firsts[block] + chunk, j * SUBLANES + m]
-                    for f in range(functions):
-                        totals[j * functions + f] += factor * values[f]
-            return tuple(totals)
-
-        totals = lax.fori_loop(0, block + 1, chunk_step, (zero,) * (SUBLANES * functions))
-        degrees = slice(block * SUBLANES, (block + 1) * SUBLANES)
-        for f in range(functions):
-            for j in range(SUBLANES):
-                c_ref[f, pl.ds(j, SUBLANES, stride=SUBLANES), :] = totals[j * functions + f]
-            energy = zero
-            for n in range(SUBLANES):
-                tile = c_ref[f, n * SUBLANES : (n + 1) * SUBLANES, :]
-                energy += tile * tile
-                held_ref[n, 0, f, degrees, :] = tile[:, :spread]
-                held_ref[n, 1, f, degrees, :] = tile[:, spread:]
-            e_ref[f, degrees, :] = energy
+        pl.when(block < first_block)(lambda: fill(block))
+        pl.when(block >= first_block)(lambda: work(block))
         out_copy(block).start()
 
     lane = lax.broadcasted_iota(jnp.int32, (SUBLANES, LANES), 1)
-    fold = jnp.where(lane % spread == 0, 1.0, 2.0).astype(jnp.bfloat16)
+    fold = jnp.where(lane == 0, 1.0, jnp.where(lane < spread, 2.0, 0.0)).astype(jnp.bfloat16)
     across = lambda part: lax.dot_general(
         fold, part, (((1,), (1,)), ((), ())), preferred_element_type=jnp.float32
     )
@@ -431,8 +468,9 @@
         rest = e_ref[f] - high.astype(jnp.float32) - low.astype(jnp.float32)
         total = across(high) + across(low) + across(rest.astype(jnp.bfloat16))
         power = jnp.where(place == f, total, power)
-    pow_ref[:, :spread] = power
-    pow_ref[:, spread:] = jnp.zeros_like(power)
+    power = jnp.concatenate([power, jnp.zeros_like(power)], axis=1)
+    for d in range(pow_ref.shape[0]):
+        pow_ref[d] = power
 
     for block in range(blocks):
         out_copy(block).wait()
@@ -440,21 +478,24 @@
 
 def degree_call(received, factors, spread):
     functions = received.shape[1]
-    tables = [*split_pair(beta_table(spread))]
-    tables += [mask.astype(jnp.bfloat16) for mask in sign_masks(spread)]
+    high, low = split_pair(beta_table(spread))
+    above = np.concatenate([high, high], axis=1)
+    below = np.concatenate([low, np.zeros_like(low)], axis=1)
+    tables = [np.concatenate([above, below], axis=0)]
+    tables += [mask.astype(np.float32) for mask in sign_masks(spread)]
     shape = (SUBLANES, 2, functions, spread, spread)
     vmem = pl.BlockSpec(memory_space=pltpu.VMEM)
     return pl.pallas_call(
         degree_kernel,
-        in_specs=[vmem] * 5 + [pl.BlockSpec(memory_space=pl.ANY)],
+        in_specs=[vmem] * 4 + [pl.BlockSpec(memory_space=pl.ANY)],
         out_specs=[pl.BlockSpec(memory_space=pl.ANY), vmem],
         out_shape=[
             jax.ShapeDtypeStruct(shape, jnp.float32),
-            jax.ShapeDtypeStruct((SUBLANES, LANES), jnp.float32),
+            jax.ShapeDtypeStruct((received.shape[0], SUBLANES, LANES), jnp.float32),
         ],
         scratch_shapes=[
-            pltpu.VMEM((functions, spread * SUBLANES, LANES), jnp.float32),
-            pltpu.VMEM((functions, SUBLANES * SUBLANES, LANES), jnp.float32),
+            pltpu.VMEM((2, functions, spread // 2 * SUBLANES, LANES), jnp.float32),
+            pltpu.VMEM((2, functions, SUBLANES * SUBLANES, LANES), jnp.float32),
             pltpu.VMEM((functions, spread, LANES), jnp.float32),
             pltpu.VMEM(shape, jnp.float32),
             pltpu.VMEM(factors.shape, jnp.float32),
@@ -476,12 +517,10 @@
     gammas, alphas = quarter_tables(spread, devices)
     alphas = lax.dynamic_index_in_dim(jnp.asarray(alphas), device, 0, keepdims=False)
     factors = factor_call(jnp.asarray(gammas), alphas)
-    coeffs, share = degree_call(received, factors, spread)
-    shares = jnp.broadcast_to(share[None], (devices,) + share.shape)
+    coeffs, shares = degree_call(received, factors, spread)
     shares = lax.all_to_all(shares, "beta", split_axis=0, concat_axis=0, tiled=True)
-    degrees = 2.0 * jnp.arange(spread, dtype=jnp.float32) + 1.0
-    energy = jnp.sum(shares[:, :functions, :spread], axis=0)
-    return coeffs, energy / (degrees * degrees)[None, :]
+    scale = (1.0 / (2.0 * np.arange(spread) + 1.0) ** 2).astype(np.float32)
+    return coeffs, jnp.sum(shares[:, :functions, :spread], axis=0) * scale[None, :]
 
 
 def local(samples):

time: 84.3 us -> 82.4 us (0.977)
  blocking collectives: 0 us -> 17.3 us
  starting transfers between devices: 18.3 us -> 8.34 us
  waiting for transfers between devices: 38.8 us -> 33 us
  Pallas kernels: 23.2 us -> 20.5 us
    all_to_all x0 -> x1, blocking collectives: none -> 17.3 us  [fast_local(): lax.all_to_all(shares, 'beta', split_axis=0, concat_axis=0, tiled=True)]
    all_to_all x1 -> x0, starting transfers between devices: 10 us -> none  [fast_local(): lax.all_to_all(shares, 'beta', split_axis=0, concat_axis=0, tiled=True)]
    all_to_all x1 -> x0, waiting for transfers between devices: 7.52 us -> none  [fast_local(): lax.all_to_all(shares, 'beta', split_axis=0, concat_axis=0, tiled=True)]
    pallas_call x1, Pallas kernels: 10.2 us -> 8.48 us  [factor_call(): pl.pallas_call(factor_kernel, out_shape=jax.ShapeDtypeStruct((steps, pair...]
    all_to_all x1, waiting for transfers between devices: 31.3 us -> 33 us  [fast_local(): lax.all_to_all(sent, 'beta', split_axis=0, concat_axis=0, tiled=True)]
    pallas_call x1, Pallas kernels: 6.98 us -> 5.93 us  [degree_call(): pl.pallas_call(degree_kernel, in_specs=[vmem] * 4 + [pl.BlockSpec(memory_...]
  transfers between devices with their start and end apart: 2 -> 1, of which waited for: 2 -> 1; matrix products, arithmetic and copies ran while one was open for 2% -> 2% of each run, Pallas kernels for 12% -> 10%
where the time goes in v3:
time: 82.4 us; the launch traced here: 82 us
  waiting for transfers between devices  33 us (40%)
  Pallas kernels  20.5 us (25%)
  blocking collectives  17.3 us (21%)
  starting transfers between devices  8.34 us (10%)
  local copies, waits for them, and re-layouts  1.54 us (2%)
    all_to_all x1, waiting for transfers between devices, fast_local(): lax.all_to_all(sent, 'beta', split_axis=0, concat_axis=0, tiled=True)  33 us
    all_to_all x1, blocking collectives, fast_local(): lax.all_to_all(shares, 'beta', split_axis=0, concat_axis=0, tiled=True)  17.3 us
    pallas_call x1, Pallas kernels, factor_call(): pl.pallas_call(factor_kernel, out_shape=jax.ShapeDtypeStruct((steps, pair...  8.48 us
    all_to_all x1, starting transfers between devices, fast_local(): lax.all_to_all(sent, 'beta', split_axis=0, concat_axis=0, tiled=True)  8.34 us
    pallas_call x1, Pallas kernels, spectrum_call(): pl.pallas_call(spectrum_kernel, grid=(functions,), in_specs=[pl.BlockSpec...  6.1 us
    pallas_call x1, Pallas kernels, degree_call(): pl.pallas_call(degree_kernel, in_specs=[vmem] * 4 + [pl.BlockSpec(memory_...  5.93 us
  transfers between devices with their start and end apart: 1, of which 1 were waited for; matrix products, arithmetic and copies ran while one was open for 2% of the time, Pallas kernels for 10%

profile of v3, /device:TPU:0, one launch (start us, length us, event | category | flops | bytes accessed | tf_op | source)
XLA Modules:
  0.0 82.0 jit_solution(3728065145149471863)
XLA Ops:
  0.6 6.1 %spectrum.1 = f32[16,4,64,128]{3,2,1,0:T(8,128)} custom-call(f32[8,4,128,128]{3,2,1,0:T(8,128)} %x_ref.1, bf16[256,256]{1,0:T(8,128)(2,1)} %constant.32.clone.gamma_two, bf16[128,256]{1,0:T(8,128)(2,1)} %constant.33.clone.gamma_lo, bf16[256,256]{1,0:T(8,128)(2,1)} %constant.34.clone.alpha_two), custom_call_target="tpu_custom_call" | custom-call | tf_op jit(solution)/shard_map/spectrum/pallas_call | solution.py:317
  6.7 8.3 %all-to-all-start = ((f32[16,4,64,128]{3,2,1,0:T(8,128)}), f32[16,4,64,128]{3,2,1,0:T(8,128)S(1)}, u32[]{:S(2)}, u32[]{:S(2)}) async-start(f32[16,4,64,128]{3,2,1,0:T(8,128)} %spectrum.1), calls=%async_computation | async-start | bytes 4194304 | tf_op jit(solution)/shard_map/all_to_all | solution.py:516
  15.1 1.5 %dynamic-slice_bitcast_fusion.alpha_ref = f32[18,8,128]{2,1,0:T(8,128)} fusion(f32[16,18,8,128]{3,2,1,0:T(8,128)} %constant.35.clone, s32[]{:T(128)S(6)} %select_n.4), kind=kLoop, calls=%fused_computation | loop fusion | bytes 147460 | tf_op jit(solution)/shard_map/jit(dynamic_index_in_dim)/squeeze | solution.py:518
  16.6 0.0 copy-start
  16.6 0.0 copy-start.1
  16.6 0.0 copy-start.2
  16.6 8.5 %factors.1.source_ref = f32[36,32,8,128]{3,2,1,0:T(8,128)} custom-call(f32[36,32,128]{2,1,0:T(8,128)} %constant.36.clone.gamma_ref, f32[18,8,128]{2,1,0:T(8,128)} %dynamic-slice_bitcast_fusion.alpha_ref), custom_call_target="tpu_custom_call" | custom-call | tf_op jit(solution)/shard_map/factors/pallas_call | solution.py:350
  25.1 0.0 copy-start.3
  25.1 33.0 %all-to-all-done.r_ref = f32[16,4,64,128]{3,2,1,0:T(8,128)S(1)} async-done(((f32[16,4,64,128]{3,2,1,0:T(8,128)}), f32[16,4,64,128]{3,2,1,0:T(8,128)S(1)}, u32[]{:S(2)}, u32[]{:S(2)}) %all-to-all-start) | async-done | bytes 2097184 | tf_op jit(solution)/shard_map/all_to_all | solution.py:516
  58.1 0.0 copy-done
  58.1 0.0 copy-done.1
  58.1 0.0 copy-done.2
  58.1 5.9 %degrees.1 = (f32[8,2,4,64,64]{4,3,2,1,0:T(8,128)}, f32[16,8,128]{2,1,0:T(8,128)S(1)}) custom-call(f32[16,4,64,128]{3,2,1,0:T(8,128)S(1)} %all-to-all-done.r_ref, bf16[256,256]{1,0:T(8,128)(2,1)S(1)} %copy-done, f32[8,128]{1,0:T(8,128)S(1)} %copy-done.2, f32[8,128]{1,0:T(8,128)S(1)} %copy-done.1, f32[36,32,8,128]{3,2,1,0:T(8,128)} %factors.1.source_ref), custom_call_target="tpu_custom_call" | custom-call | tf_op jit(solution)/shard_map/degrees/pallas_call | solution.py:488
  64.1 17.3 %all_to_all.10 = f32[16,8,128]{2,1,0:T(8,128)S(1)} all-to-all(f32[16,8,128]{2,1,0:T(8,128)S(1)} %get-tuple-element.5), channel_id=1, replica_groups=mesh['beta'=16,'grp'=2] {'beta'}, dimensions={0} | all-to-all | bytes 131072 | tf_op jit(solution)/shard_map/all_to_all | solution.py:521
  81.4 0.0 copy-done.3
  81.4 0.6 broadcast_multiply_fusion
  (1 shorter events, 0.0 us)
Async XLA Ops:
  6.7 51.4 %all-to-all-start = ((f32[16,4,64,128]{3,2,1,0:T(8,128)}), f32[16,4,64,128]{3,2,1,0:T(8,128)S(1)}, u32[]{:S(2)}, u32[]{:S(2)}) async-start(f32[16,4,64,128]{3,2,1,0:T(8,128)} %spectrum.1), calls=%async_computation | async-start | bytes 4194304 | tf_op jit(solution)/shard_map/all_to_all | solution.py:516
  16.6 41.5 %copy-start = (bf16[256,256]{1,0:T(8,128)(2,1)S(1)}, bf16[256,256]{1,0:T(8,128)(2,1)}, u32[]{:S(2)}) copy-start(bf16[256,256]{1,0:T(8,128)(2,1)} %constant.37.clone.beta_two) | copy-start | bytes 393220
  16.6 41.5 %copy-start.1 = (f32[8,128]{1,0:T(8,128)S(1)}, f32[8,128]{1,0:T(8,128)}, u32[]{:S(2)}) copy-start(f32[8,128]{1,0:T(8,128)} %constant.39.clone.odd_ref) | copy-start | bytes 12292
  16.6 41.5 %copy-start.2 = (f32[8,128]{1,0:T(8,128)S(1)}, f32[8,128]{1,0:T(8,128)}, u32[]{:S(2)}) copy-start(f32[8,128]{1,0:T(8,128)} %constant.38.clone.even_ref) | copy-start | bytes 12292
  25.1 56.3 %copy-start.3 = (f32[64]{0:T(128)S(1)}, f32[64]{0:T(128)}, u32[]{:S(2)}) copy-start(f32[64]{0:T(128)} %constant.42) | copy-start | bytes 772

commit v4 on v3

--- a/solution.py
+++ b/solution.py
@@ -518,7 +518,10 @@
     alphas = lax.dynamic_index_in_dim(jnp.asarray(alphas), device, 0, keepdims=False)
     factors = factor_call(jnp.asarray(gammas), alphas)
     coeffs, shares = degree_call(received, factors, spread)
-    shares = lax.all_to_all(shares, "beta", split_axis=0, concat_axis=0, tiled=True)
+    order = list(range(devices))[::-1]
+    shares = lax.all_to_all(
+        shares, "beta", split_axis=0, concat_axis=0, tiled=True, axis_index_groups=[order]
+    )
     scale = (1.0 / (2.0 * np.arange(spread) + 1.0) ** 2).astype(np.float32)
     return coeffs, jnp.sum(shares[:, :functions, :spread], axis=0) * scale[None, :]
 

time: 82.4 us -> 79 us (0.959)
  blocking collectives: 17.3 us -> 14 us
    all_to_all x1, blocking collectives: 17.3 us -> 14 us  [fast_local(): lax.all_to_all(shares, 'beta', split_axis=0, concat_axis=0, tiled=True, a...]
  transfers between devices with their start and end apart: 1 -> 1, of which waited for: 1 -> 1; matrix products, arithmetic and copies ran while one was open for 2% -> 2% of each run, Pallas kernels for 10% -> 11%
where the time goes in v4:
time: 79 us; the launch traced here: 78.7 us
  waiting for transfers between devices  33 us (42%)
  Pallas kernels  20.5 us (26%)
  blocking collectives  14 us (18%)
  starting transfers between devices  8.34 us (11%)
  local copies, waits for them, and re-layouts  1.54 us (2%)
    all_to_all x1, waiting for transfers between devices, fast_local(): lax.all_to_all(sent, 'beta', split_axis=0, concat_axis=0, tiled=True)  33 us
    all_to_all x1, blocking collectives, fast_local(): lax.all_to_all(shares, 'beta', split_axis=0, concat_axis=0, tiled=True, a...  14 us
    pallas_call x1, Pallas kernels, factor_call(): pl.pallas_call(factor_kernel, out_shape=jax.ShapeDtypeStruct((steps, pair...  8.48 us
    all_to_all x1, starting transfers between devices, fast_local(): lax.all_to_all(sent, 'beta', split_axis=0, concat_axis=0, tiled=True)  8.34 us
    pallas_call x1, Pallas kernels, spectrum_call(): pl.pallas_call(spectrum_kernel, grid=(functions,), in_specs=[pl.BlockSpec...  6.1 us
    pallas_call x1, Pallas kernels, degree_call(): pl.pallas_call(degree_kernel, in_specs=[vmem] * 4 + [pl.BlockSpec(memory_...  5.93 us
  transfers between devices with their start and end apart: 1, of which 1 were waited for; matrix products, arithmetic and copies ran while one was open for 2% of the time, Pallas kernels for 11%

profile of v4, /device:TPU:0, one launch (start us, length us, event | category | flops | bytes accessed | tf_op | source)
XLA Modules:
  0.0 78.7 jit_solution(6748013461803849057)
XLA Ops:
  0.6 6.1 %spectrum.1 = f32[16,4,64,128]{3,2,1,0:T(8,128)} custom-call(f32[8,4,128,128]{3,2,1,0:T(8,128)} %x_ref.1, bf16[256,256]{1,0:T(8,128)(2,1)} %constant.32.clone.gamma_two, bf16[128,256]{1,0:T(8,128)(2,1)} %constant.33.clone.gamma_lo, bf16[256,256]{1,0:T(8,128)(2,1)} %constant.34.clone.alpha_two), custom_call_target="tpu_custom_call" | custom-call | tf_op jit(solution)/shard_map/spectrum/pallas_call | solution.py:317
  6.7 8.3 %all-to-all-start = ((f32[16,4,64,128]{3,2,1,0:T(8,128)}), f32[16,4,64,128]{3,2,1,0:T(8,128)S(1)}, u32[]{:S(2)}, u32[]{:S(2)}) async-start(f32[16,4,64,128]{3,2,1,0:T(8,128)} %spectrum.1), calls=%async_computation | async-start | bytes 4194304 | tf_op jit(solution)/shard_map/all_to_all | solution.py:516
  15.1 1.5 %dynamic-slice_bitcast_fusion.alpha_ref = f32[18,8,128]{2,1,0:T(8,128)} fusion(f32[16,18,8,128]{3,2,1,0:T(8,128)} %constant.35.clone, s32[]{:T(128)S(6)} %select_n.4), kind=kLoop, calls=%fused_computation | loop fusion | bytes 147460 | tf_op jit(solution)/shard_map/jit(dynamic_index_in_dim)/squeeze | solution.py:518
  16.6 0.0 copy-start
  16.6 0.0 copy-start.1
  16.6 0.0 copy-start.2
  16.6 8.5 %factors.1.source_ref = f32[36,32,8,128]{3,2,1,0:T(8,128)} custom-call(f32[36,32,128]{2,1,0:T(8,128)} %constant.36.clone.gamma_ref, f32[18,8,128]{2,1,0:T(8,128)} %dynamic-slice_bitcast_fusion.alpha_ref), custom_call_target="tpu_custom_call" | custom-call | tf_op jit(solution)/shard_map/factors/pallas_call | solution.py:350
  25.1 0.0 copy-start.3
  25.1 33.0 %all-to-all-done.r_ref = f32[16,4,64,128]{3,2,1,0:T(8,128)S(1)} async-done(((f32[16,4,64,128]{3,2,1,0:T(8,128)}), f32[16,4,64,128]{3,2,1,0:T(8,128)S(1)}, u32[]{:S(2)}, u32[]{:S(2)}) %all-to-all-start) | async-done | bytes 2097184 | tf_op jit(solution)/shard_map/all_to_all | solution.py:516
  58.1 0.0 copy-done
  58.1 0.0 copy-done.1
  58.1 0.0 copy-done.2
  58.1 5.9 %degrees.1 = (f32[8,2,4,64,64]{4,3,2,1,0:T(8,128)}, f32[16,8,128]{2,1,0:T(8,128)S(1)}) custom-call(f32[16,4,64,128]{3,2,1,0:T(8,128)S(1)} %all-to-all-done.r_ref, bf16[256,256]{1,0:T(8,128)(2,1)S(1)} %copy-done, f32[8,128]{1,0:T(8,128)S(1)} %copy-done.2, f32[8,128]{1,0:T(8,128)S(1)} %copy-done.1, f32[36,32,8,128]{3,2,1,0:T(8,128)} %factors.1.source_ref), custom_call_target="tpu_custom_call" | custom-call | tf_op jit(solution)/shard_map/degrees/pallas_call | solution.py:488
  64.1 14.0 %all_to_all.10 = f32[16,8,128]{2,1,0:T(8,128)S(1)} all-to-all(f32[16,8,128]{2,1,0:T(8,128)S(1)} %get-tuple-element.5), channel_id=1, replica_groups={{30,28,26,24,22,20,18,16,14,12,10,8,6,4,2,0},{31,29,27,25,23,21,19,17,1..., dimensions={0} | all-to-all | bytes 131072 | tf_op jit(solution)/shard_map/all_to_all | solution.py:522
  78.1 0.0 copy-done.3
  78.1 0.6 broadcast_multiply_fusion
  (1 shorter events, 0.0 us)
Async XLA Ops:
  6.7 51.4 %all-to-all-start = ((f32[16,4,64,128]{3,2,1,0:T(8,128)}), f32[16,4,64,128]{3,2,1,0:T(8,128)S(1)}, u32[]{:S(2)}, u32[]{:S(2)}) async-start(f32[16,4,64,128]{3,2,1,0:T(8,128)} %spectrum.1), calls=%async_computation | async-start | bytes 4194304 | tf_op jit(solution)/shard_map/all_to_all | solution.py:516
  16.6 41.5 %copy-start = (bf16[256,256]{1,0:T(8,128)(2,1)S(1)}, bf16[256,256]{1,0:T(8,128)(2,1)}, u32[]{:S(2)}) copy-start(bf16[256,256]{1,0:T(8,128)(2,1)} %constant.37.clone.beta_two) | copy-start | bytes 393220
  16.6 41.5 %copy-start.1 = (f32[8,128]{1,0:T(8,128)S(1)}, f32[8,128]{1,0:T(8,128)}, u32[]{:S(2)}) copy-start(f32[8,128]{1,0:T(8,128)} %constant.39.clone.odd_ref) | copy-start | bytes 12292
  16.6 41.5 %copy-start.2 = (f32[8,128]{1,0:T(8,128)S(1)}, f32[8,128]{1,0:T(8,128)}, u32[]{:S(2)}) copy-start(f32[8,128]{1,0:T(8,128)} %constant.38.clone.even_ref) | copy-start | bytes 12292
  25.1 53.0 %copy-start.3 = (f32[64]{0:T(128)S(1)}, f32[64]{0:T(128)}, u32[]{:S(2)}) copy-start(f32[64]{0:T(128)} %constant.42) | copy-start | bytes 772

commit v5 on v4

--- a/solution.py
+++ b/solution.py
@@ -225,7 +225,7 @@
     at = np.arange(grid)
     phase = 2.0 * np.pi / grid * (at[:, None] * np.arange(spread)[None, :] % grid)
     cosine, sine = np.cos(phase), -np.sin(phase)
-    gamma_part = np.concatenate([cosine, sine, sine, -cosine], axis=1)
+    gamma_part = np.concatenate([cosine, sine], axis=1)
     phase = 2.0 * np.pi / grid * (at[:, None] * at[None, :] % grid)
     alpha_part = np.concatenate([np.cos(phase), np.sin(phase)], axis=1) / grid
     return gamma_part, alpha_part
@@ -282,21 +282,28 @@
     return jnp.dot(left, right, preferred_element_type=jnp.float32)
 
 
-def spectrum_kernel(x_ref, gamma_two, gamma_lo, alpha_two, out_ref):
+def quarter_turn(value):
+    middle = value.shape[1] // 2
+    return jnp.concatenate([value[:, middle:], -value[:, :middle]], axis=1)
+
+
+def spectrum_kernel(x_ref, gamma_two, alpha_two, out_ref):
     count, _, grid, _ = x_ref.shape
     blocks = out_ref.shape[0]
     high, low = split_value(x_ref[:, 0].reshape(count * grid, grid))
-    half = dot(jnp.concatenate([high, low], axis=1), gamma_two[...]) + dot(high, gamma_lo[...])
+    both = dot(jnp.concatenate([high, low], axis=1), gamma_two[...])
+    halves = split_value(both[:, :LANES] + both[:, LANES:])
     for k in range(0, count, 2):
-        pairs = [half[(k + i) * grid : (k + i + 1) * grid] for i in range(2)]
-        pair = jnp.concatenate(
-            [
-                jnp.concatenate([p[:, :LANES] for p in pairs], axis=1),
-                jnp.concatenate([p[:, LANES:] for p in pairs], axis=1),
-            ],
-            axis=0,
-        )
-        high, low = split_value(pair)
+        high, low = [
+            jnp.concatenate(
+                [
+                    jnp.concatenate([turn(part[(k + i) * grid : (k + i + 1) * grid]) for i in range(2)], axis=1)
+                    for turn in (lambda value: value, quarter_turn)
+                ],
+                axis=0,
+            )
+            for part in halves
+        ]
         both = dot(alpha_two[...], high)
         rows = both[:grid] + both[grid:] + dot(alpha_two[:grid], low)
         for i in range(2):
@@ -310,7 +317,9 @@
     count, functions, grid, _ = samples.shape
     gamma_part, alpha_part = fourier_tables(grid // 2)
     gamma_hi, gamma_lo = split_pair(gamma_part)
-    tables = [np.concatenate([gamma_hi, gamma_hi], axis=0), gamma_lo]
+    above = np.concatenate([gamma_hi, gamma_lo], axis=1)
+    below = np.concatenate([gamma_hi, np.zeros_like(gamma_lo)], axis=1)
+    tables = [np.concatenate([above, below], axis=0)]
     tables.append(np.concatenate(split_pair(alpha_part), axis=0))
     rows = grid // devices * count
     whole = lambda table: pl.BlockSpec(table.shape, lambda f: (0, 0))

time: 79 us -> 78.3 us (level)
  no operation moved by 1% of the time
where the time goes in v5:
time: 78.3 us; the launch traced here: 78 us
  waiting for transfers between devices  33 us (42%)
  Pallas kernels  19.8 us (25%)
  blocking collectives  14 us (18%)
  starting transfers between devices  8.34 us (11%)
  local copies, waits for them, and re-layouts  1.54 us (2%)
    all_to_all x1, waiting for transfers between devices, fast_local(): lax.all_to_all(sent, 'beta', split_axis=0, concat_axis=0, tiled=True)  33 us
    all_to_all x1, blocking collectives, fast_local(): lax.all_to_all(shares, 'beta', split_axis=0, concat_axis=0, tiled=True, a...  14 us
    pallas_call x1, Pallas kernels, factor_call(): pl.pallas_call(factor_kernel, out_shape=jax.ShapeDtypeStruct((steps, pair...  8.48 us
    all_to_all x1, starting transfers between devices, fast_local(): lax.all_to_all(sent, 'beta', split_axis=0, concat_axis=0, tiled=True)  8.34 us
    pallas_call x1, Pallas kernels, degree_call(): pl.pallas_call(degree_kernel, in_specs=[vmem] * 4 + [pl.BlockSpec(memory_...  5.93 us
    pallas_call x1, Pallas kernels, spectrum_call(): pl.pallas_call(spectrum_kernel, grid=(functions,), in_specs=[pl.BlockSpec...  5.38 us
  transfers between devices with their start and end apart: 1, of which 1 were waited for; matrix products, arithmetic and copies ran while one was open for 2% of the time, Pallas kernels for 11%

profile of v5, /device:TPU:0, one launch (start us, length us, event | category | flops | bytes accessed | tf_op | source)
XLA Modules:
  0.0 78.0 jit_solution(9962605463358157049)
XLA Ops:
  0.6 5.4 %spectrum.1 = f32[16,4,64,128]{3,2,1,0:T(8,128)} custom-call(f32[8,4,128,128]{3,2,1,0:T(8,128)} %x_ref.1, bf16[256,256]{1,0:T(8,128)(2,1)} %constant.30.clone.gamma_two, bf16[256,256]{1,0:T(8,128)(2,1)} %constant.31.clone.alpha_two), custom_call_target="tpu_custom_call" | custom-call | tf_op jit(solution)/shard_map/spectrum/pallas_call | solution.py:326
  6.0 8.3 %all-to-all-start = ((f32[16,4,64,128]{3,2,1,0:T(8,128)}), f32[16,4,64,128]{3,2,1,0:T(8,128)S(1)}, u32[]{:S(2)}, u32[]{:S(2)}) async-start(f32[16,4,64,128]{3,2,1,0:T(8,128)} %spectrum.1), calls=%async_computation | async-start | bytes 4194304 | tf_op jit(solution)/shard_map/all_to_all | solution.py:525
  14.4 1.5 %dynamic-slice_bitcast_fusion.alpha_ref = f32[18,8,128]{2,1,0:T(8,128)} fusion(f32[16,18,8,128]{3,2,1,0:T(8,128)} %constant.32.clone, s32[]{:T(128)S(6)} %select_n.4), kind=kLoop, calls=%fused_computation | loop fusion | bytes 147460 | tf_op jit(solution)/shard_map/jit(dynamic_index_in_dim)/squeeze | solution.py:527
  15.9 0.0 copy-start
  15.9 0.0 copy-start.1
  15.9 0.0 copy-start.2
  15.9 8.5 %factors.1.source_ref = f32[36,32,8,128]{3,2,1,0:T(8,128)} custom-call(f32[36,32,128]{2,1,0:T(8,128)} %constant.33.clone.gamma_ref, f32[18,8,128]{2,1,0:T(8,128)} %dynamic-slice_bitcast_fusion.alpha_ref), custom_call_target="tpu_custom_call" | custom-call | tf_op jit(solution)/shard_map/factors/pallas_call | solution.py:359
  24.4 0.0 copy-start.3
  24.4 33.0 %all-to-all-done.r_ref = f32[16,4,64,128]{3,2,1,0:T(8,128)S(1)} async-done(((f32[16,4,64,128]{3,2,1,0:T(8,128)}), f32[16,4,64,128]{3,2,1,0:T(8,128)S(1)}, u32[]{:S(2)}, u32[]{:S(2)}) %all-to-all-start) | async-done | bytes 2097184 | tf_op jit(solution)/shard_map/all_to_all | solution.py:525
  57.4 0.0 copy-done
  57.4 0.0 copy-done.1
  57.4 0.0 copy-done.2
  57.4 5.9 %degrees.1 = (f32[8,2,4,64,64]{4,3,2,1,0:T(8,128)}, f32[16,8,128]{2,1,0:T(8,128)S(1)}) custom-call(f32[16,4,64,128]{3,2,1,0:T(8,128)S(1)} %all-to-all-done.r_ref, bf16[256,256]{1,0:T(8,128)(2,1)S(1)} %copy-done, f32[8,128]{1,0:T(8,128)S(1)} %copy-done.2, f32[8,128]{1,0:T(8,128)S(1)} %copy-done.1, f32[36,32,8,128]{3,2,1,0:T(8,128)} %factors.1.source_ref), custom_call_target="tpu_custom_call" | custom-call | tf_op jit(solution)/shard_map/degrees/pallas_call | solution.py:497
  63.3 14.0 %all_to_all.10 = f32[16,8,128]{2,1,0:T(8,128)S(1)} all-to-all(f32[16,8,128]{2,1,0:T(8,128)S(1)} %get-tuple-element.5), channel_id=1, replica_groups={{30,28,26,24,22,20,18,16,14,12,10,8,6,4,2,0},{31,29,27,25,23,21,19,17,1..., dimensions={0} | all-to-all | bytes 131072 | tf_op jit(solution)/shard_map/all_to_all | solution.py:531
  77.4 0.0 copy-done.3
  77.4 0.6 broadcast_multiply_fusion
  (1 shorter events, 0.0 us)
Async XLA Ops:
  6.0 51.4 %all-to-all-start = ((f32[16,4,64,128]{3,2,1,0:T(8,128)}), f32[16,4,64,128]{3,2,1,0:T(8,128)S(1)}, u32[]{:S(2)}, u32[]{:S(2)}) async-start(f32[16,4,64,128]{3,2,1,0:T(8,128)} %spectrum.1), calls=%async_computation | async-start | bytes 4194304 | tf_op jit(solution)/shard_map/all_to_all | solution.py:525
  15.9 41.5 %copy-start = (bf16[256,256]{1,0:T(8,128)(2,1)S(1)}, bf16[256,256]{1,0:T(8,128)(2,1)}, u32[]{:S(2)}) copy-start(bf16[256,256]{1,0:T(8,128)(2,1)} %constant.34.clone.beta_two) | copy-start | bytes 393220
  15.9 41.5 %copy-start.1 = (f32[8,128]{1,0:T(8,128)S(1)}, f32[8,128]{1,0:T(8,128)}, u32[]{:S(2)}) copy-start(f32[8,128]{1,0:T(8,128)} %constant.36.clone.odd_ref) | copy-start | bytes 12292
  15.9 41.5 %copy-start.2 = (f32[8,128]{1,0:T(8,128)S(1)}, f32[8,128]{1,0:T(8,128)}, u32[]{:S(2)}) copy-start(f32[8,128]{1,0:T(8,128)} %constant.35.clone.even_ref) | copy-start | bytes 12292
  24.4 53.0 %copy-start.3 = (f32[64]{0:T(128)S(1)}, f32[64]{0:T(128)}, u32[]{:S(2)}) copy-start(f32[64]{0:T(128)} %constant.39) | copy-start | bytes 772

commit v6 on v5

--- a/solution.py
+++ b/solution.py
@@ -282,35 +282,32 @@
     return jnp.dot(left, right, preferred_element_type=jnp.float32)
 
 
-def quarter_turn(value):
-    middle = value.shape[1] // 2
-    return jnp.concatenate([value[:, middle:], -value[:, :middle]], axis=1)
-
-
 def spectrum_kernel(x_ref, gamma_two, alpha_two, out_ref):
     count, _, grid, _ = x_ref.shape
     blocks = out_ref.shape[0]
-    high, low = split_value(x_ref[:, 0].reshape(count * grid, grid))
-    both = dot(jnp.concatenate([high, low], axis=1), gamma_two[...])
-    halves = split_value(both[:, :LANES] + both[:, LANES:])
-    for k in range(0, count, 2):
-        high, low = [
-            jnp.concatenate(
+    for f in range(x_ref.shape[1]):
+        high, low = split_value(x_ref[:, f].reshape(count * grid, grid))
+        both = dot(jnp.concatenate([high, low], axis=1), gamma_two[...])
+        half = both[:, :LANES] + both[:, LANES:]
+        lane = lax.broadcasted_iota(jnp.int32, (1, LANES), 1)
+        sign = jnp.where(lane < LANES // 2, 1.0, -1.0)
+        for k in range(0, count, 2):
+            pairs = [half[(k + i) * grid : (k + i + 1) * grid] for i in range(2)]
+            pair = jnp.concatenate(
                 [
-                    jnp.concatenate([turn(part[(k + i) * grid : (k + i + 1) * grid]) for i in range(2)], axis=1)
-                    for turn in (lambda value: value, quarter_turn)
+                    jnp.concatenate(pairs, axis=1),
+                    jnp.concatenate([pltpu.roll(p, LANES // 2, 1) * sign for p in pairs], axis=1),
                 ],
                 axis=0,
             )
-            for part in halves
-        ]
-        both = dot(alpha_two[...], high)
-        rows = both[:grid] + both[grid:] + dot(alpha_two[:grid], low)
-        for i in range(2):
-            for d in range(blocks):
-                out_ref[d, 0, pl.ds(k + i, SUBLANES, stride=count), :] = rows[
-                    d * SUBLANES : (d + 1) * SUBLANES, i * LANES : (i + 1) * LANES
-                ]
+            high, low = split_value(pair)
+            both = dot(alpha_two[...], high)
+            rows = both[:grid] + both[grid:] + dot(alpha_two[:grid], low)
+            for i in range(2):
+                for d in range(blocks):
+                    out_ref[d, f, pl.ds(k + i, SUBLANES, stride=count), :] = rows[
+                        d * SUBLANES : (d + 1) * SUBLANES, i * LANES : (i + 1) * LANES
+                    ]
 
 
 def spectrum_call(samples, devices):
@@ -322,13 +319,15 @@
     tables = [np.concatenate([above, below], axis=0)]
     tables.append(np.concatenate(split_pair(alpha_part), axis=0))
     rows = grid // devices * count
+    steps = 2
+    some = functions // steps
     whole = lambda table: pl.BlockSpec(table.shape, lambda f: (0, 0))
     return pl.pallas_call(
         spectrum_kernel,
-        grid=(functions,),
-        in_specs=[pl.BlockSpec((count, 1, grid, grid), lambda f: (0, f, 0, 0))]
+        grid=(steps,),
+        in_specs=[pl.BlockSpec((count, some, grid, grid), lambda f: (0, f, 0, 0))]
         + [whole(table) for table in tables],
-        out_specs=pl.BlockSpec((devices, 1, rows, LANES), lambda f: (0, f, 0, 0)),
+        out_specs=pl.BlockSpec((devices, some, rows, LANES), lambda f: (0, f, 0, 0)),
         out_shape=jax.ShapeDtypeStruct((devices, functions, rows, LANES), jnp.float32),
         name="spectrum",
     )(samples, *tables)

time: 78.3 us -> 77.8 us (level)
  no operation moved by 1% of the time
where the time goes in v6:
time: 77.8 us; the launch traced here: 77.5 us
  waiting for transfers between devices  33 us (42%)
  Pallas kernels  19.3 us (25%)
  blocking collectives  14 us (18%)
  starting transfers between devices  8.34 us (11%)
  local copies, waits for them, and re-layouts  1.54 us (2%)
    all_to_all x1, waiting for transfers between devices, fast_local(): lax.all_to_all(sent, 'beta', split_axis=0, concat_axis=0, tiled=True)  33 us
    all_to_all x1, blocking collectives, fast_local(): lax.all_to_all(shares, 'beta', split_axis=0, concat_axis=0, tiled=True, a...  14 us
    pallas_call x1, Pallas kernels, factor_call(): pl.pallas_call(factor_kernel, out_shape=jax.ShapeDtypeStruct((steps, pair...  8.48 us
    all_to_all x1, starting transfers between devices, fast_local(): lax.all_to_all(sent, 'beta', split_axis=0, concat_axis=0, tiled=True)  8.34 us
    pallas_call x1, Pallas kernels, degree_call(): pl.pallas_call(degree_kernel, in_specs=[vmem] * 4 + [pl.BlockSpec(memory_...  5.93 us
    pallas_call x1, Pallas kernels, spectrum_call(): pl.pallas_call(spectrum_kernel, grid=(steps,), in_specs=[pl.BlockSpec((co...  4.9 us
  transfers between devices with their start and end apart: 1, of which 1 were waited for; matrix products, arithmetic and copies ran while one was open for 2% of the time, Pallas kernels for 11%

profile of v6, /device:TPU:0, one launch (start us, length us, event | category | flops | bytes accessed | tf_op | source)
XLA Modules:
  0.0 77.5 jit_solution(17563779429307192016)
XLA Ops:
  0.6 4.9 %spectrum.1 = f32[16,4,64,128]{3,2,1,0:T(8,128)} custom-call(f32[8,4,128,128]{3,2,1,0:T(8,128)} %x_ref.1, bf16[256,256]{1,0:T(8,128)(2,1)} %constant.30.clone.gamma_two, bf16[256,256]{1,0:T(8,128)(2,1)} %constant.31.clone.alpha_two), custom_call_target="tpu_custom_call" | custom-call | tf_op jit(solution)/shard_map/spectrum/pallas_call | solution.py:325
  5.5 8.3 %all-to-all-start = ((f32[16,4,64,128]{3,2,1,0:T(8,128)}), f32[16,4,64,128]{3,2,1,0:T(8,128)S(1)}, u32[]{:S(2)}, u32[]{:S(2)}) async-start(f32[16,4,64,128]{3,2,1,0:T(8,128)} %spectrum.1), calls=%async_computation | async-start | bytes 4194304 | tf_op jit(solution)/shard_map/all_to_all | solution.py:524
  13.9 1.5 %dynamic-slice_bitcast_fusion.alpha_ref = f32[18,8,128]{2,1,0:T(8,128)} fusion(f32[16,18,8,128]{3,2,1,0:T(8,128)} %constant.32.clone, s32[]{:T(128)S(6)} %select_n.4), kind=kLoop, calls=%fused_computation | loop fusion | bytes 147460 | tf_op jit(solution)/shard_map/jit(dynamic_index_in_dim)/squeeze | solution.py:526
  15.4 0.0 copy-start
  15.4 0.0 copy-start.1
  15.4 0.0 copy-start.2
  15.4 8.5 %factors.1.source_ref = f32[36,32,8,128]{3,2,1,0:T(8,128)} custom-call(f32[36,32,128]{2,1,0:T(8,128)} %constant.33.clone.gamma_ref, f32[18,8,128]{2,1,0:T(8,128)} %dynamic-slice_bitcast_fusion.alpha_ref), custom_call_target="tpu_custom_call" | custom-call | tf_op jit(solution)/shard_map/factors/pallas_call | solution.py:358
  23.9 0.0 copy-start.3
  23.9 33.0 %all-to-all-done.r_ref = f32[16,4,64,128]{3,2,1,0:T(8,128)S(1)} async-done(((f32[16,4,64,128]{3,2,1,0:T(8,128)}), f32[16,4,64,128]{3,2,1,0:T(8,128)S(1)}, u32[]{:S(2)}, u32[]{:S(2)}) %all-to-all-start) | async-done | bytes 2097184 | tf_op jit(solution)/shard_map/all_to_all | solution.py:524
  56.9 0.0 copy-done
  56.9 0.0 copy-done.1
  56.9 0.0 copy-done.2
  56.9 5.9 %degrees.1 = (f32[8,2,4,64,64]{4,3,2,1,0:T(8,128)}, f32[16,8,128]{2,1,0:T(8,128)S(1)}) custom-call(f32[16,4,64,128]{3,2,1,0:T(8,128)S(1)} %all-to-all-done.r_ref, bf16[256,256]{1,0:T(8,128)(2,1)S(1)} %copy-done, f32[8,128]{1,0:T(8,128)S(1)} %copy-done.2, f32[8,128]{1,0:T(8,128)S(1)} %copy-done.1, f32[36,32,8,128]{3,2,1,0:T(8,128)} %factors.1.source_ref), custom_call_target="tpu_custom_call" | custom-call | tf_op jit(solution)/shard_map/degrees/pallas_call | solution.py:496
  62.9 14.0 %all_to_all.10 = f32[16,8,128]{2,1,0:T(8,128)S(1)} all-to-all(f32[16,8,128]{2,1,0:T(8,128)S(1)} %get-tuple-element.5), channel_id=1, replica_groups={{30,28,26,24,22,20,18,16,14,12,10,8,6,4,2,0},{31,29,27,25,23,21,19,17,1..., dimensions={0} | all-to-all | bytes 131072 | tf_op jit(solution)/shard_map/all_to_all | solution.py:530
  76.9 0.0 copy-done.3
  76.9 0.6 broadcast_multiply_fusion
  (1 shorter events, 0.0 us)
Async XLA Ops:
  5.5 51.4 %all-to-all-start = ((f32[16,4,64,128]{3,2,1,0:T(8,128)}), f32[16,4,64,128]{3,2,1,0:T(8,128)S(1)}, u32[]{:S(2)}, u32[]{:S(2)}) async-start(f32[16,4,64,128]{3,2,1,0:T(8,128)} %spectrum.1), calls=%async_computation | async-start | bytes 4194304 | tf_op jit(solution)/shard_map/all_to_all | solution.py:524
  15.4 41.5 %copy-start = (bf16[256,256]{1,0:T(8,128)(2,1)S(1)}, bf16[256,256]{1,0:T(8,128)(2,1)}, u32[]{:S(2)}) copy-start(bf16[256,256]{1,0:T(8,128)(2,1)} %constant.34.clone.beta_two) | copy-start | bytes 393220
  15.4 41.5 %copy-start.1 = (f32[8,128]{1,0:T(8,128)S(1)}, f32[8,128]{1,0:T(8,128)}, u32[]{:S(2)}) copy-start(f32[8,128]{1,0:T(8,128)} %constant.36.clone.odd_ref) | copy-start | bytes 12292
  15.4 41.5 %copy-start.2 = (f32[8,128]{1,0:T(8,128)S(1)}, f32[8,128]{1,0:T(8,128)}, u32[]{:S(2)}) copy-start(f32[8,128]{1,0:T(8,128)} %constant.35.clone.even_ref) | copy-start | bytes 12292
  23.9 53.0 %copy-start.3 = (f32[64]{0:T(128)S(1)}, f32[64]{0:T(128)}, u32[]{:S(2)}) copy-start(f32[64]{0:T(128)} %constant.39) | copy-start | bytes 772

commit v7 on v6

--- a/solution.py
+++ b/solution.py
@@ -346,7 +346,7 @@
                     jnp.broadcast_to(column[:, lane + j : lane + j + 1], (SUBLANES, LANES))
                     for j in range(2)
                 ]
-                row = gamma_ref[2 * at + half, pl.ds(i, SUBLANES, stride=0), :]
+                row = gamma_ref[2 * at + half, i : i + 1, :]
                 out_ref[2 * at + half, i] = jnp.where(left, wide[0], wide[1]) * row
         return carry
 
@@ -478,7 +478,7 @@
         power = jnp.where(place == f, total, power)
     power = jnp.concatenate([power, jnp.zeros_like(power)], axis=1)
     for d in range(pow_ref.shape[0]):
-        pow_ref[d] = power
+        pow_ref[d] = power[:functions]
 
     for block in range(blocks):
         out_copy(block).wait()
@@ -499,7 +499,7 @@
         out_specs=[pl.BlockSpec(memory_space=pl.ANY), vmem],
         out_shape=[
             jax.ShapeDtypeStruct(shape, jnp.float32),
-            jax.ShapeDtypeStruct((received.shape[0], SUBLANES, LANES), jnp.float32),
+            jax.ShapeDtypeStruct((received.shape[0], functions, LANES), jnp.float32),
         ],
         scratch_shapes=[
             pltpu.VMEM((2, functions, spread // 2 * SUBLANES, LANES), jnp.float32),
@@ -531,7 +531,7 @@
         shares, "beta", split_axis=0, concat_axis=0, tiled=True, axis_index_groups=[order]
     )
     scale = (1.0 / (2.0 * np.arange(spread) + 1.0) ** 2).astype(np.float32)
-    return coeffs, jnp.sum(shares[:, :functions, :spread], axis=0) * scale[None, :]
+    return coeffs, jnp.sum(shares[:, :, :spread], axis=0) * scale[None, :]
 
 
 def local(samples):

time: 77.8 us -> 77.5 us (level)
  no operation moved by 1% of the time
where the time goes in v7:
time: 77.5 us; the launch traced here: 77.1 us
  waiting for transfers between devices  33 us (43%)
  Pallas kernels  19.3 us (25%)
  blocking collectives  13.7 us (18%)
  starting transfers between devices  8.34 us (11%)
  local copies, waits for them, and re-layouts  1.54 us (2%)
    all_to_all x1, waiting for transfers between devices, fast_local(): lax.all_to_all(sent, 'beta', split_axis=0, concat_axis=0, tiled=True)  33 us
    all_to_all x1, blocking collectives, fast_local(): lax.all_to_all(shares, 'beta', split_axis=0, concat_axis=0, tiled=True, a...  13.7 us
    pallas_call x1, Pallas kernels, factor_call(): pl.pallas_call(factor_kernel, out_shape=jax.ShapeDtypeStruct((steps, pair...  8.48 us
    all_to_all x1, starting transfers between devices, fast_local(): lax.all_to_all(sent, 'beta', split_axis=0, concat_axis=0, tiled=True)  8.34 us
    pallas_call x1, Pallas kernels, degree_call(): pl.pallas_call(degree_kernel, in_specs=[vmem] * 4 + [pl.BlockSpec(memory_...  5.93 us
    pallas_call x1, Pallas kernels, spectrum_call(): pl.pallas_call(spectrum_kernel, grid=(steps,), in_specs=[pl.BlockSpec((co...  4.9 us
  transfers between devices with their start and end apart: 1, of which 1 were waited for; matrix products, arithmetic and copies ran while one was open for 2% of the time, Pallas kernels for 11%

profile of v7, /device:TPU:0, one launch (start us, length us, event | category | flops | bytes accessed | tf_op | source)
XLA Modules:
  0.0 77.1 jit_solution(9152129169238445679)
XLA Ops:
  0.6 4.9 %spectrum.1 = f32[16,4,64,128]{3,2,1,0:T(8,128)} custom-call(f32[8,4,128,128]{3,2,1,0:T(8,128)} %x_ref.1, bf16[256,256]{1,0:T(8,128)(2,1)} %constant.30.clone.gamma_two, bf16[256,256]{1,0:T(8,128)(2,1)} %constant.31.clone.alpha_two), custom_call_target="tpu_custom_call" | custom-call | tf_op jit(solution)/shard_map/spectrum/pallas_call | solution.py:325
  5.5 8.3 %all-to-all-start = ((f32[16,4,64,128]{3,2,1,0:T(8,128)}), f32[16,4,64,128]{3,2,1,0:T(8,128)S(1)}, u32[]{:S(2)}, u32[]{:S(2)}) async-start(f32[16,4,64,128]{3,2,1,0:T(8,128)} %spectrum.1), calls=%async_computation | async-start | bytes 4194304 | tf_op jit(solution)/shard_map/all_to_all | solution.py:524
  13.9 1.5 %dynamic-slice_bitcast_fusion.alpha_ref = f32[18,8,128]{2,1,0:T(8,128)} fusion(f32[16,18,8,128]{3,2,1,0:T(8,128)} %constant.32.clone, s32[]{:T(128)S(6)} %select_n.4), kind=kLoop, calls=%fused_computation | loop fusion | bytes 147460 | tf_op jit(solution)/shard_map/jit(dynamic_index_in_dim)/squeeze | solution.py:526
  15.4 0.0 copy-start
  15.4 0.0 copy-start.1
  15.4 0.0 copy-start.2
  15.4 8.5 %factors.1.source_ref = f32[36,32,8,128]{3,2,1,0:T(8,128)} custom-call(f32[36,32,128]{2,1,0:T(8,128)} %constant.33.clone.gamma_ref, f32[18,8,128]{2,1,0:T(8,128)} %dynamic-slice_bitcast_fusion.alpha_ref), custom_call_target="tpu_custom_call" | custom-call | tf_op jit(solution)/shard_map/factors/pallas_call | solution.py:358
  23.9 0.0 copy-start.3
  23.9 33.0 %all-to-all-done.r_ref = f32[16,4,64,128]{3,2,1,0:T(8,128)S(1)} async-done(((f32[16,4,64,128]{3,2,1,0:T(8,128)}), f32[16,4,64,128]{3,2,1,0:T(8,128)S(1)}, u32[]{:S(2)}, u32[]{:S(2)}) %all-to-all-start) | async-done | bytes 2097184 | tf_op jit(solution)/shard_map/all_to_all | solution.py:524
  56.9 0.0 copy-done
  56.9 0.0 copy-done.1
  56.9 0.0 copy-done.2
  56.9 5.9 %degrees.1 = (f32[8,2,4,64,64]{4,3,2,1,0:T(8,128)}, f32[16,4,128]{2,1,0:T(4,128)S(1)}) custom-call(f32[16,4,64,128]{3,2,1,0:T(8,128)S(1)} %all-to-all-done.r_ref, bf16[256,256]{1,0:T(8,128)(2,1)S(1)} %copy-done, f32[8,128]{1,0:T(8,128)S(1)} %copy-done.2, f32[8,128]{1,0:T(8,128)S(1)} %copy-done.1, f32[36,32,8,128]{3,2,1,0:T(8,128)} %factors.1.source_ref), custom_call_target="tpu_custom_call" | custom-call | tf_op jit(solution)/shard_map/degrees/pallas_call | solution.py:496
  62.9 13.7 %all_to_all.10 = f32[16,4,128]{2,1,0:T(4,128)S(1)} all-to-all(f32[16,4,128]{2,1,0:T(4,128)S(1)} %get-tuple-element.5), channel_id=1, replica_groups={{30,28,26,24,22,20,18,16,14,12,10,8,6,4,2,0},{31,29,27,25,23,21,19,17,1..., dimensions={0} | all-to-all | bytes 65536 | tf_op jit(solution)/shard_map/all_to_all | solution.py:530
  76.6 0.0 copy-done.3
  76.6 0.6 broadcast_multiply_fusion
  (1 shorter events, 0.0 us)
Async XLA Ops:
  5.5 51.4 %all-to-all-start = ((f32[16,4,64,128]{3,2,1,0:T(8,128)}), f32[16,4,64,128]{3,2,1,0:T(8,128)S(1)}, u32[]{:S(2)}, u32[]{:S(2)}) async-start(f32[16,4,64,128]{3,2,1,0:T(8,128)} %spectrum.1), calls=%async_computation | async-start | bytes 4194304 | tf_op jit(solution)/shard_map/all_to_all | solution.py:524
  15.4 41.5 %copy-start = (bf16[256,256]{1,0:T(8,128)(2,1)S(1)}, bf16[256,256]{1,0:T(8,128)(2,1)}, u32[]{:S(2)}) copy-start(bf16[256,256]{1,0:T(8,128)(2,1)} %constant.34.clone.beta_two) | copy-start | bytes 393220
  15.4 41.5 %copy-start.1 = (f32[8,128]{1,0:T(8,128)S(1)}, f32[8,128]{1,0:T(8,128)}, u32[]{:S(2)}) copy-start(f32[8,128]{1,0:T(8,128)} %constant.36.clone.odd_ref) | copy-start | bytes 12292
  15.4 41.5 %copy-start.2 = (f32[8,128]{1,0:T(8,128)S(1)}, f32[8,128]{1,0:T(8,128)}, u32[]{:S(2)}) copy-start(f32[8,128]{1,0:T(8,128)} %constant.35.clone.even_ref) | copy-start | bytes 12292
  23.9 52.7 %copy-start.3 = (f32[64]{0:T(128)S(1)}, f32[64]{0:T(128)}, u32[]{:S(2)}) copy-start(f32[64]{0:T(128)} %constant.39) | copy-start | bytes 772

commit v8 on v7

--- a/solution.py
+++ b/solution.py
@@ -282,9 +282,13 @@
     return jnp.dot(left, right, preferred_element_type=jnp.float32)
 
 
+def data_order(devices):
+    return [(place + devices // 2) % devices for place in range(devices)]
+
+
 def spectrum_kernel(x_ref, gamma_two, alpha_two, out_ref):
     count, _, grid, _ = x_ref.shape
-    blocks = out_ref.shape[0]
+    order = data_order(out_ref.shape[0])
     for f in range(x_ref.shape[1]):
         high, low = split_value(x_ref[:, f].reshape(count * grid, grid))
         both = dot(jnp.concatenate([high, low], axis=1), gamma_two[...])
@@ -304,8 +308,8 @@
             both = dot(alpha_two[...], high)
             rows = both[:grid] + both[grid:] + dot(alpha_two[:grid], low)
             for i in range(2):
-                for d in range(blocks):
-                    out_ref[d, f, pl.ds(k + i, SUBLANES, stride=count), :] = rows[
+                for place, d in enumerate(order):
+                    out_ref[place, f, pl.ds(k + i, SUBLANES, stride=count), :] = rows[
                         d * SUBLANES : (d + 1) * SUBLANES, i * LANES : (i + 1) * LANES
                     ]
 
@@ -486,7 +490,9 @@
 
 def degree_call(received, factors, spread):
     functions = received.shape[1]
-    high, low = split_pair(beta_table(spread))
+    sources = received.shape[0]
+    table = beta_table(spread).reshape(2 * spread, sources, -1)[:, data_order(sources)]
+    high, low = split_pair(table.reshape(2 * spread, 2 * spread))
     above = np.concatenate([high, high], axis=1)
     below = np.concatenate([low, np.zeros_like(low)], axis=1)
     tables = [np.concatenate([above, below], axis=0)]
@@ -521,7 +527,9 @@
     functions, grid_size = samples.shape[1:3]
     spread = grid_size // 2
     sent = spectrum_call(samples, devices)
-    received = lax.all_to_all(sent, "beta", split_axis=0, concat_axis=0, tiled=True)
+    received = lax.all_to_all(
+        sent, "beta", split_axis=0, concat_axis=0, tiled=True, axis_index_groups=[data_order(devices)]
+    )
     gammas, alphas = quarter_tables(spread, devices)
     alphas = lax.dynamic_index_in_dim(jnp.asarray(alphas), device, 0, keepdims=False)
     factors = factor_call(jnp.asarray(gammas), alphas)

time: 77.5 us -> 76.3 us (0.985)
  waiting for transfers between devices: 33 us -> 30.3 us
  blocking collectives: 13.7 us -> 14.8 us
    all_to_all x1, waiting for transfers between devices: 33 us -> 30.3 us  [fast_local(): lax.all_to_all(sent, 'beta', split_axis=0, concat_axis=0, tiled=True, axi...]
    all_to_all x1, blocking collectives: 13.7 us -> 14.8 us  [fast_local(): lax.all_to_all(shares, 'beta', split_axis=0, concat_axis=0, tiled=True, a...]
where the time goes in v8:
time: 76.3 us; the launch traced here: 76 us
  waiting for transfers between devices  30.3 us (40%)
  Pallas kernels  19.3 us (25%)
  blocking collectives  14.8 us (19%)
  starting transfers between devices  8.81 us (12%)
  local copies, waits for them, and re-layouts  1.54 us (2%)
    all_to_all x1, waiting for transfers between devices, fast_local(): lax.all_to_all(sent, 'beta', split_axis=0, concat_axis=0, tiled=True, axi...  30.3 us
    all_to_all x1, blocking collectives, fast_local(): lax.all_to_all(shares, 'beta', split_axis=0, concat_axis=0, tiled=True, a...  14.8 us
    all_to_all x1, starting transfers between devices, fast_local(): lax.all_to_all(sent, 'beta', split_axis=0, concat_axis=0, tiled=True, axi...  8.81 us
    pallas_call x1, Pallas kernels, factor_call(): pl.pallas_call(factor_kernel, out_shape=jax.ShapeDtypeStruct((steps, pair...  8.48 us
    pallas_call x1, Pallas kernels, degree_call(): pl.pallas_call(degree_kernel, in_specs=[vmem] * 4 + [pl.BlockSpec(memory_...  5.93 us
    pallas_call x1, Pallas kernels, spectrum_call(): pl.pallas_call(spectrum_kernel, grid=(steps,), in_specs=[pl.BlockSpec((co...  4.9 us
  transfers between devices with their start and end apart: 1, of which 1 were waited for; matrix products, arithmetic and copies ran while one was open for 2% of the time, Pallas kernels for 11%

profile of v8, /device:TPU:0, one launch (start us, length us, event | category | flops | bytes accessed | tf_op | source)
XLA Modules:
  0.0 76.0 jit_solution(4031467553773170405)
XLA Ops:
  0.6 4.9 %spectrum.1 = f32[16,4,64,128]{3,2,1,0:T(8,128)} custom-call(f32[8,4,128,128]{3,2,1,0:T(8,128)} %x_ref.1, bf16[256,256]{1,0:T(8,128)(2,1)} %constant.30.clone.gamma_two, bf16[256,256]{1,0:T(8,128)(2,1)} %constant.31.clone.alpha_two), custom_call_target="tpu_custom_call" | custom-call | tf_op jit(solution)/shard_map/spectrum/pallas_call | solution.py:329
  5.5 8.8 %all-to-all-start = ((f32[16,4,64,128]{3,2,1,0:T(8,128)}), f32[16,4,64,128]{3,2,1,0:T(8,128)S(1)}, u32[]{:S(2)}, u32[]{:S(2)}) async-start(f32[16,4,64,128]{3,2,1,0:T(8,128)} %spectrum.1), calls=%async_computation | async-start | bytes 4194304 | tf_op jit(solution)/shard_map/all_to_all | solution.py:530
  14.3 1.5 %dynamic-slice_bitcast_fusion.alpha_ref = f32[18,8,128]{2,1,0:T(8,128)} fusion(f32[16,18,8,128]{3,2,1,0:T(8,128)} %constant.32.clone, s32[]{:T(128)S(6)} %select_n.4), kind=kLoop, calls=%fused_computation | loop fusion | bytes 147460 | tf_op jit(solution)/shard_map/jit(dynamic_index_in_dim)/squeeze | solution.py:534
  15.9 0.0 copy-start
  15.9 0.0 copy-start.1
  15.9 0.0 copy-start.2
  15.9 8.5 %factors.1.source_ref = f32[36,32,8,128]{3,2,1,0:T(8,128)} custom-call(f32[36,32,128]{2,1,0:T(8,128)} %constant.33.clone.gamma_ref, f32[18,8,128]{2,1,0:T(8,128)} %dynamic-slice_bitcast_fusion.alpha_ref), custom_call_target="tpu_custom_call" | custom-call | tf_op jit(solution)/shard_map/factors/pallas_call | solution.py:362
  24.4 0.0 copy-start.3
  24.4 30.3 %all-to-all-done.r_ref = f32[16,4,64,128]{3,2,1,0:T(8,128)S(1)} async-done(((f32[16,4,64,128]{3,2,1,0:T(8,128)}), f32[16,4,64,128]{3,2,1,0:T(8,128)S(1)}, u32[]{:S(2)}, u32[]{:S(2)}) %all-to-all-start) | async-done | bytes 2097184 | tf_op jit(solution)/shard_map/all_to_all | solution.py:530
  54.6 0.0 copy-done
  54.6 0.0 copy-done.1
  54.6 0.0 copy-done.2
  54.6 5.9 %degrees.1 = (f32[8,2,4,64,64]{4,3,2,1,0:T(8,128)}, f32[16,4,128]{2,1,0:T(4,128)S(1)}) custom-call(f32[16,4,64,128]{3,2,1,0:T(8,128)S(1)} %all-to-all-done.r_ref, bf16[256,256]{1,0:T(8,128)(2,1)S(1)} %copy-done, f32[8,128]{1,0:T(8,128)S(1)} %copy-done.2, f32[8,128]{1,0:T(8,128)S(1)} %copy-done.1, f32[36,32,8,128]{3,2,1,0:T(8,128)} %factors.1.source_ref), custom_call_target="tpu_custom_call" | custom-call | tf_op jit(solution)/shard_map/degrees/pallas_call | solution.py:502
  60.6 14.8 %all_to_all.10 = f32[16,4,128]{2,1,0:T(4,128)S(1)} all-to-all(f32[16,4,128]{2,1,0:T(4,128)S(1)} %get-tuple-element.5), channel_id=1, replica_groups={{30,28,26,24,22,20,18,16,14,12,10,8,6,4,2,0},{31,29,27,25,23,21,19,17,1..., dimensions={0} | all-to-all | bytes 65536 | tf_op jit(solution)/shard_map/all_to_all | solution.py:538
  75.4 0.0 copy-done.3
  75.4 0.6 broadcast_multiply_fusion
  (1 shorter events, 0.0 us)
Async XLA Ops:
  5.5 49.1 %all-to-all-start = ((f32[16,4,64,128]{3,2,1,0:T(8,128)}), f32[16,4,64,128]{3,2,1,0:T(8,128)S(1)}, u32[]{:S(2)}, u32[]{:S(2)}) async-start(f32[16,4,64,128]{3,2,1,0:T(8,128)} %spectrum.1), calls=%async_computation | async-start | bytes 4194304 | tf_op jit(solution)/shard_map/all_to_all | solution.py:530
  15.9 38.8 %copy-start = (bf16[256,256]{1,0:T(8,128)(2,1)S(1)}, bf16[256,256]{1,0:T(8,128)(2,1)}, u32[]{:S(2)}) copy-start(bf16[256,256]{1,0:T(8,128)(2,1)} %constant.34.clone.beta_two) | copy-start | bytes 393220
  15.9 38.8 %copy-start.1 = (f32[8,128]{1,0:T(8,128)S(1)}, f32[8,128]{1,0:T(8,128)}, u32[]{:S(2)}) copy-start(f32[8,128]{1,0:T(8,128)} %constant.36.clone.odd_ref) | copy-start | bytes 12292
  15.9 38.8 %copy-start.2 = (f32[8,128]{1,0:T(8,128)S(1)}, f32[8,128]{1,0:T(8,128)}, u32[]{:S(2)}) copy-start(f32[8,128]{1,0:T(8,128)} %constant.35.clone.even_ref) | copy-start | bytes 12292
  24.4 51.0 %copy-start.3 = (f32[64]{0:T(128)S(1)}, f32[64]{0:T(128)}, u32[]{:S(2)}) copy-start(f32[64]{0:T(128)} %constant.39) | copy-start | bytes 772
